TPU v7x, 32 devices: a 4x2x2 block of a 4x4x8 slice. The times are simulated.
32 devices in a mesh: dp: 4 (over y, z), cp: 8 (over x, core).
Axes of the slice: x: 4, y: 2, z: 2, core: 2. Of those that a mesh axis runs over, the one named last changes fastest.
The devices are a block of a 4x4x8 slice.
Arguments:
- x_act: bfloat16 [8, 1024, 3584], P('dp', 'cp'), parts along dimension 0
- d_out: bfloat16 [8, 1024, 3584], P('dp', 'cp'), parts along dimension 0
- positions: int32 [8, 1024], P('dp', 'cp'), parts along dimension 0
- ln_gain: float32 [3584], replicated
- ln_bias: float32 [3584], replicated
- w_query: bfloat16 [3584, 28, 128], replicated
- w_key: bfloat16 [3584, 4, 128], replicated
- w_value: bfloat16 [3584, 4, 128], replicated
- w_out: bfloat16 [3584, 3584], replicated
Outputs:
- output 1: bfloat16 [8, 1024, 3584], P('dp', 'cp'), parts along dimension 0
- output 2: bfloat16 [8, 1024, 3584], P('dp', 'cp'), parts along dimension 0
- output 3: float32 [14336, 28, 128], P(('dp', 'cp')), parts along dimension 0
- output 4: float32 [14336, 4, 128], P(('dp', 'cp')), parts along dimension 0
- output 5: float32 [14336, 4, 128], P(('dp', 'cp')), parts along dimension 0
- output 6: float32 [14336, 3584], P(('dp', 'cp')), parts along dimension 0
- output 7: float32 [14336], P('dp'), parts along dimension 0
- output 8: float32 [14336], P('dp'), parts along dimension 0
There are 4 independent parts. A program takes and returns all parts, laid end to end along the dimension named above; an argument that names none is the same for every part.
All inputs are finite; a program needn't handle non-finite values.
Results may differ from a plain program's by a relative error of at most 0.00671658.
Values are sent between devices in bfloat16 or wider.
A program may use at most 768 MiB of HBM per device.

v0:
```python
import math
import jax
import jax.numpy as jnp
from jax import lax
from jax.sharding import PartitionSpec as P

EPS = 1e-5
ROPE_BASE = 10000.0
Q_TILE = 128


def norm_forward(x_act, ln_gain, ln_bias):
    x_f32 = x_act.astype(jnp.float32)
    centered = x_f32 - jnp.mean(x_f32, axis=-1, keepdims=True)
    inv_std = lax.rsqrt(jnp.mean(centered * centered, axis=-1, keepdims=True) + EPS)
    x_hat = centered * inv_std
    return (x_hat * (1.0 + ln_gain) + ln_bias).astype(jnp.bfloat16), x_hat, inv_std


def norm_backward(grad_h, x_hat, inv_std, ln_gain):
    grad_hat = grad_h * (1.0 + ln_gain)
    mean_one = jnp.mean(grad_hat, axis=-1, keepdims=True)
    mean_two = jnp.mean(grad_hat * x_hat, axis=-1, keepdims=True)
    return inv_std * (grad_hat - mean_one - x_hat * mean_two)


def rope_tables(positions, head_dim):
    quarter = head_dim // 4
    freq_tab = jnp.exp(jnp.arange(quarter, dtype=jnp.float32) * (-2.0 * math.log(ROPE_BASE) / (head_dim // 2)))
    angles = positions.astype(jnp.float32)[..., None] * freq_tab
    return jnp.cos(angles)[..., None, :], jnp.sin(angles)[..., None, :]


def rope_rotate(values, cos_tab, sin_tab):
    quarter = cos_tab.shape[-1]
    first_half = values[..., :quarter]
    second_half = values[..., quarter:2 * quarter]
    return jnp.concatenate([first_half * cos_tab - second_half * sin_tab, second_half * cos_tab + first_half * sin_tab, values[..., 2 * quarter:]], axis=-1)


def tile_probs(q_tile, key_all, q_first):
    head_dim = q_tile.shape[-1]
    scores = jnp.einsum('bqkgd,blkd->bkgql', q_tile, key_all, preferred_element_type=jnp.float32) * (head_dim ** -0.5)
    q_index = q_first + jnp.arange(q_tile.shape[1])
    k_index = jnp.arange(key_all.shape[1])
    scores = jnp.where(k_index[None, :] <= q_index[:, None], scores, -1e30)
    shifted = jnp.exp(scores - jnp.max(scores, axis=-1, keepdims=True))
    return shifted / jnp.sum(shifted, axis=-1, keepdims=True)


def attention_forward(q_grouped, key_all, value_all, q_base):
    n_batch, seq_len = q_grouped.shape[0], q_grouped.shape[1]

    def one_tile(tile_idx):
        q_first = tile_idx * Q_TILE
        q_tile = lax.dynamic_slice_in_dim(q_grouped, q_first, Q_TILE, axis=1)
        tile_prob = tile_probs(q_tile, key_all, q_base + q_first)
        tile_mix = jnp.einsum('bkgql,blkd->bqkgd', tile_prob.astype(jnp.bfloat16), value_all, preferred_element_type=jnp.float32)
        return tile_mix.astype(jnp.bfloat16)

    out_tiles = lax.map(one_tile, jnp.arange(seq_len // Q_TILE))
    return jnp.moveaxis(out_tiles, 0, 1).reshape(n_batch * seq_len, -1)


def attention_backward(q_grouped, key_all, value_all, grad_attn, q_base):
    n_batch, seq_len = q_grouped.shape[0], q_grouped.shape[1]
    head_dim = q_grouped.shape[-1]

    def one_tile(acc_pair, tile_idx):
        grad_k, grad_v = acc_pair
        q_first = tile_idx * Q_TILE
        q_tile = lax.dynamic_slice_in_dim(q_grouped, q_first, Q_TILE, axis=1)
        ga_tile = lax.dynamic_slice_in_dim(grad_attn, q_first, Q_TILE, axis=1)
        tile_prob = tile_probs(q_tile, key_all, q_base + q_first)
        grad_prob = jnp.einsum('bqkgd,blkd->bkgql', ga_tile, value_all, preferred_element_type=jnp.float32)
        row_dot = jnp.sum(tile_prob * grad_prob, axis=-1, keepdims=True)
        grad_score = (tile_prob * (grad_prob - row_dot) * (head_dim ** -0.5)).astype(jnp.bfloat16)
        grad_q = jnp.einsum('bkgql,blkd->bqkgd', grad_score, key_all, preferred_element_type=jnp.float32)
        grad_k = grad_k + jnp.einsum('bkgql,bqkgd->blkd', grad_score, q_tile, preferred_element_type=jnp.float32)
        grad_v = grad_v + jnp.einsum('bkgql,bqkgd->blkd', tile_prob.astype(jnp.bfloat16), ga_tile, preferred_element_type=jnp.float32)
        return (grad_k, grad_v), grad_q

    zero_acc = jnp.zeros(key_all.shape, jnp.float32)
    (grad_k, grad_v), q_tiles = lax.scan(one_tile, (zero_acc, zero_acc), jnp.arange(seq_len // Q_TILE))
    grad_q = jnp.moveaxis(q_tiles, 0, 1).reshape(n_batch, seq_len, -1, head_dim)
    return grad_q, grad_k, grad_v


def reduce_rows(values):
    return lax.psum_scatter(values, 'cp', scatter_dimension=0, tiled=True)


def solution(mesh):
    def device_step(x_act, d_out, positions, ln_gain, ln_bias, w_query, w_key, w_value, w_out):
        n_batch, seq_len, n_width = x_act.shape
        q_heads = w_query.shape[1]
        kv_heads, head_dim = w_key.shape[1], w_key.shape[2]
        n_tokens = n_batch * seq_len
        q_base = lax.axis_index('cp') * seq_len
        normed, x_hat, inv_std = norm_forward(x_act, ln_gain, ln_bias)
        flat_h = normed.reshape(n_tokens, n_width)
        cos_tab, sin_tab = rope_tables(positions, head_dim)
        q_act = rope_rotate(jnp.einsum('td,dnh->tnh', flat_h, w_query, preferred_element_type=jnp.float32).reshape(n_batch, seq_len, q_heads, head_dim), cos_tab, sin_tab).astype(jnp.bfloat16)
        k_act = rope_rotate(jnp.einsum('td,dnh->tnh', flat_h, w_key, preferred_element_type=jnp.float32).reshape(n_batch, seq_len, kv_heads, head_dim), cos_tab, sin_tab).astype(jnp.bfloat16)
        v_act = jnp.einsum('td,dnh->tnh', flat_h, w_value, preferred_element_type=jnp.float32).astype(jnp.bfloat16).reshape(n_batch, seq_len, kv_heads, head_dim)
        q_grouped = q_act.reshape(n_batch, seq_len, kv_heads, q_heads // kv_heads, head_dim)
        key_all = lax.all_gather(k_act, 'cp', axis=1, tiled=True)
        value_all = lax.all_gather(v_act, 'cp', axis=1, tiled=True)
        attn_act = attention_forward(q_grouped, key_all, value_all, q_base)
        block_out = (x_act.astype(jnp.float32) + jnp.dot(attn_act, w_out, preferred_element_type=jnp.float32).reshape(n_batch, seq_len, n_width)).astype(jnp.bfloat16)
        grad_flat = d_out.reshape(n_tokens, n_width)
        grad_wo = jnp.einsum('tn,td->nd', attn_act, grad_flat, preferred_element_type=jnp.float32)
        grad_attn = jnp.einsum('td,nd->tn', grad_flat, w_out, preferred_element_type=jnp.float32).astype(jnp.bfloat16).reshape(q_grouped.shape)
        kv_again = lax.all_gather(jnp.stack([k_act, v_act]), 'cp', axis=2, tiled=True)
        grad_q, grad_k_all, grad_v_all = attention_backward(q_grouped, kv_again[0], kv_again[1], grad_attn, q_base)
        grad_k_own = lax.psum_scatter(grad_k_all, 'cp', scatter_dimension=1, tiled=True)
        grad_v_own = lax.psum_scatter(grad_v_all, 'cp', scatter_dimension=1, tiled=True)
        grad_q_pre = rope_rotate(grad_q, cos_tab, -sin_tab).astype(jnp.bfloat16).reshape(n_tokens, q_heads, head_dim)
        grad_k_pre = rope_rotate(grad_k_own, cos_tab, -sin_tab).astype(jnp.bfloat16).reshape(n_tokens, kv_heads, head_dim)
        grad_v_pre = grad_v_own.astype(jnp.bfloat16).reshape(n_tokens, kv_heads, head_dim)
        grad_h = (jnp.einsum('tnh,dnh->td', grad_q_pre, w_query, preferred_element_type=jnp.float32) + jnp.einsum('tnh,dnh->td', grad_k_pre, w_key, preferred_element_type=jnp.float32) + jnp.einsum('tnh,dnh->td', grad_v_pre, w_value, preferred_element_type=jnp.float32)).reshape(n_batch, seq_len, n_width)
        grad_wq = jnp.einsum('td,tnh->dnh', flat_h, grad_q_pre, preferred_element_type=jnp.float32)
        grad_wk = jnp.einsum('td,tnh->dnh', flat_h, grad_k_pre, preferred_element_type=jnp.float32)
        grad_wv = jnp.einsum('td,tnh->dnh', flat_h, grad_v_pre, preferred_element_type=jnp.float32)
        grad_x = (d_out.astype(jnp.float32) + norm_backward(grad_h, x_hat, inv_std, ln_gain)).astype(jnp.bfloat16)
        grad_gain = lax.psum(jnp.sum(grad_h * x_hat, axis=(0, 1)), 'cp')
        grad_bias = lax.psum(jnp.sum(grad_h, axis=(0, 1)), 'cp')
        return (block_out, grad_x, reduce_rows(grad_wq), reduce_rows(grad_wk), reduce_rows(grad_wv), reduce_rows(grad_wo), grad_gain, grad_bias)

    return jax.shard_map(device_step, mesh=mesh, in_specs=(P('dp', 'cp', None), P('dp', 'cp', None), P('dp', 'cp'), P(None), P(None), P(None, None, None), P(None, None, None), P(None, None, None), P(None, None)), out_specs=(P('dp', 'cp', None), P('dp', 'cp', None), P(('dp', 'cp'), None, None), P(('dp', 'cp'), None, None), P(('dp', 'cp'), None, None), P(('dp', 'cp'), None), P('dp'), P('dp')), check_vma=False)
```

profile of v0, /device:TPU:81, one launch (start us, length us, event | category | flops | bytes accessed | tf_op | source)
XLA Modules:
  0.0 886.7 jit_solution(5372750128161325354)
XLA Ops:
  7.3 1.8 convert_reduce_fusion
  9.1 2.1 fusion.45
  11.3 7.0 copy.48
  20.4 1.1 fusion.46
  21.6 1.7 copy-done.7
  26.4 16.7 %fusion.8 = f32[2,128,28,128]{1,3,2,0:T(8,128)} fusion(bf16[3584,28,128]{2,0,1:T(8,128)(2,1)} %param.14, bf16[2,128,3584]{2,1,0:T(8,128)(2,1)} %copy-done.10), kind=kOutput, calls=%fused_computation.16 | convolution fusion | flops 6576668672 | bytes 31195136 | tf_op jit(solution)/shard_map/td,dnh->tnh/dot_general | solution.py:103
  43.1 1.7 slice.110
  44.8 2.5 subtract_convert_fusion.1
  47.3 2.7 copy.50
  50.0 1.6 copy.51
  51.6 1.6 copy.52
  53.2 13.3 %convolution_convert_fusion = bf16[256,3584]{1,0:T(8,128)(2,1)} fusion(bf16[256,3584]{1,0:T(8,128)(2,1)S(1)} %bitcast.240, bf16[3584,3584]{1,0:T(8,128)(2,1)} %param.17), kind=kOutput, calls=%fused_computation.44 | convolution fusion | flops 6577586176 | bytes 29360128 | tf_op jit(solution)/shard_map/td,nd->tn/dot_general | solution.py:113
  66.5 4.7 reshape.186
  71.2 3.5 copy.77
  74.7 5.5 pad_maximum_fusion
  80.4 15.3 %fusion.59 = f32[2,4,1024,128,7]{3,2,4,1,0:T(8,128)} fusion(bf16[2,128,4,7,128]{1,4,3,2,0:T(8,128)(2,1)S(1)} %copy.77, bf16[2,2,1024,4,128]{2,4,3,1,0:T(8,128)(2,1)} %all-gather.8.cloned.1.call-done), kind=kOutput, calls=%fused_computation.71 | convolution fusion | flops 1879048192 | bytes 33292288 | tf_op jit(solution)/shard_map/while/body/eval_jaxpr/bqkgd,blkd->bkgql/dot_general | solution.py:75
  95.7 16.5 %fusion.126 = (f32[2,4,7,128]{3,2,1,0:T(8,128)S(1)}, f32[2,4,7,128,1024]{3,4,2,1,0:T(8,128)}) fusion(pred[128,1024]{0,1:T(8,128)(4,1)S(1)} %iota_compare_fusion, bf16[2,128,4,7,128]{4,1,3,2,0:T(8,128)(2,1)} %pad_maximum_fusion, bf16[2,2,1024,4,128]{2,4,3,1,0:T(8,128)(2,1)} %all-gather.8.cloned.1.call-done), kind=kOutput, calls=%fused_computation.148 | convolution fusion | flops 1908409344 | bytes 33452032 | tf_op jit(solution)/shard_map/while/body/eval_jaxpr/sub | solution.py:47
  112.1 39.8 %fusion.55 = f32[2,1024,4,128]{1,3,2,0:T(8,128)} fusion(bf16[2,128,4,7,128]{4,1,3,2,0:T(8,128)(2,1)} %pad_maximum_fusion, f32[2,4,1024,128,7]{3,2,4,1,0:T(8,128)} %fusion.59, f32[2,4,7,128,1024]{3,4,2,1,0:T(8,128)} %get-tuple-element.89, f32[2,4,7,128]{3,2,1,0:T(8,128)S(1)} %get-tuple-element.88), kind=kOutput, calls=%fused_computation.68 | convolution fusion | flops 1930436608 | bytes 64778240 | tf_op jit(solution)/shard_map/while/body/eval_jaxpr/bkgql,bqkgd->blkd/dot_general | solution.py:79
  152.1 16.3 %fusion.56 = f32[2,1024,4,128]{1,3,2,0:T(8,128)} fusion(bf16[2,128,4,7,128]{1,4,3,2,0:T(8,128)(2,1)S(1)} %copy.77, f32[2,4,7,128]{3,2,1,0:T(8,128)S(1)} %get-tuple-element.88, pred[128,1024]{0,1:T(8,128)(4,1)S(1)} %iota_compare_fusion, bf16[2,128,4,7,128]{4,1,3,2,0:T(8,128)(2,1)} %pad_maximum_fusion, ...), kind=kOutput, calls=%fused_computation.69 | convolution fusion | flops 3794804736 | bytes 10121216 | tf_op jit(solution)/shard_map/while/body/eval_jaxpr/bkgql,bqkgd->blkd/dot_general | solution.py:80
  171.4 16.8 %reduce-scatter.7.cloned.1.call-done = f32[2,128,4,128]{1,3,2,0:T(8,128)} async-done(((f32[2,1024,4,128]{1,3,2,0:T(8,128)}), f32[2,128,4,128]{1,3,2,0:T(8,128)}) %reduce-scatter.7.cloned.1.call-update) | async-done | bytes 524304 | tf_op jit(solution)/shard_map/reduce_scatter | solution.py:116
  190.3 4.1 convolution_bitcast_fusion.2
  194.5 30.4 %reduce-scatter.9.cloned.1.call-done = f32[2,128,4,128]{1,3,2,0:T(8,128)} async-done(((f32[2,1024,4,128]{1,3,2,0:T(8,128)}), f32[2,128,4,128]{1,3,2,0:T(8,128)}) %reduce-scatter.9.cloned.1.call-update) | async-done | bytes 524304 | tf_op jit(solution)/shard_map/reduce_scatter | solution.py:117
  226.7 4.1 convolution_bitcast_fusion.1
  230.9 21.5 %all-gather.6.cloned.1.call-done = bf16[2,1024,4,128]{1,3,2,0:T(8,128)(2,1)} async-done(((bf16[2,128,4,128]{1,3,2,0:T(8,128)(2,1)}), bf16[2,1024,4,128]{1,3,2,0:T(8,128)(2,1)}) %all-gather.6.cloned.1.call-update) | async-done | bytes 2097168 | tf_op jit(solution)/shard_map/all_gather | solution.py:107
  252.5 16.5 %fusion.121 = (f32[2,4,7,128]{3,2,1,0:T(8,128)S(1)}, f32[2,4,7,128,1024]{3,4,2,1,0:T(8,128)}) fusion(pred[128,1024]{0,1:T(8,128)(4,1)S(1)} %iota_compare_fusion, bf16[2,128,4,7,128]{4,1,3,2,0:T(8,128)(2,1)S(1)} %copy-done.9, bf16[2,1024,4,128]{1,3,2,0:T(8,128)(2,1)} %all-gather.6.cloned.1.call-done), kind=kOutput, calls=%fused_computation.147 | convolution fusion | flops 1908409344 | bytes 33452032 | tf_op jit(solution)/shard_map/while/body/eval_jaxpr/sub | solution.py:47
  269.0 9.7 %all-gather.4.cloned.1.call-done = bf16[2,1024,4,128]{1,3,2,0:T(8,128)(2,1)} async-done(((bf16[2,128,4,128]{1,3,2,0:T(8,128)(2,1)}), bf16[2,1024,4,128]{1,3,2,0:T(8,128)(2,1)}) %all-gather.4.cloned.1.call-update) | async-done | bytes 2097168 | tf_op jit(solution)/shard_map/all_gather | solution.py:108
  278.7 12.8 %fusion.86 = bf16[2,4,128,7,128]{4,2,3,1,0:T(8,128)(2,1)S(1)} fusion(f32[2,4,7,128,1024]{3,4,2,1,0:T(8,128)} %get-tuple-element.87, f32[2,4,7,128]{3,2,1,0:T(8,128)S(1)} %get-tuple-element.86, bf16[2,1024,4,128]{1,3,2,0:T(8,128)(2,1)} %all-gather.4.cloned.1.call-done), kind=kOutput, calls=%fused_computation.98 | convolution fusion | flops 1894645760 | bytes 33320960 | tf_op jit(solution)/shard_map/while/body/eval_jaxpr/bkgql,blkd->bqkgd/dot_general | solution.py:58
  291.5 3.2 copy.87
  294.7 21.5 %fusion.68 = f32[3584,3584]{1,0:T(8,128)} fusion(bf16[256,3584]{1,0:T(8,128)(2,1)} %bitcast.239, bf16[448,8,2,128]{3,2,1,0:T(2,128)(2,1)} %bitcast.238), kind=kOutput, calls=%fused_computation.77 | convolution fusion | flops 6576668672 | bytes 55050240 | tf_op jit(solution)/shard_map/tn,td->nd/dot_general | solution.py:112
  316.3 39.2 %fusion.23 = f32[2,4,128,7,128]{4,2,3,1,0:T(8,128)} fusion(f32[2,4,1024,128,7]{3,2,4,1,0:T(8,128)} %fusion.59, bf16[2,2,1024,4,128]{2,4,3,1,0:T(8,128)(2,1)} %all-gather.8.cloned.1.call-done, f32[2,4,7,128,1024]{3,4,2,1,0:T(8,128)} %get-tuple-element.89, f32[2,4,7,128]{3,2,1,0:T(8,128)S(1)} %get-tuple-element.88), kind=kOutput, calls=%fused_computation.32 | convolution fusion | flops 1930436608 | bytes 123273216 | tf_op jit(solution)/shard_map/while/body/eval_jaxpr/bkgql,blkd->bqkgd/dot_general | solution.py:78
  355.6 1.8 slice.109
  357.4 2.5 subtract_convert_fusion
  359.9 19.5 %convolution_bitcast_fusion = f32[3584,28,128]{2,0,1:T(8,128)} fusion(bf16[2,128,28,64]{1,3,2,0:T(8,128)(2,1)S(1)} %slice.109, bf16[2,128,28,32]{1,3,2,0:T(8,128)(2,1)S(1)} %get-tuple-element.76, bf16[2,128,28,32]{1,3,2,0:T(8,128)(2,1)} %get-tuple-element.75, bf16[2,128,3584]{2,1,0:T(8,128)(2,1)S(1)} %copy-done.12), kind=kOutput, calls=%fused_computation.3 | convolution fusion | flops 6582173696 | bytes 55050240 | tf_op jit(solution)/shard_map/td,tnh->dnh/dot_general | solution.py:122
  379.4 1.4 copy-done.1
  380.9 13.3 %fusion.28 = bf16[2,128,3584]{2,1,0:T(8,128)(2,1)} fusion(bf16[2,128,3584]{1,2,0:T(8,128)(2,1)} %bitcast.237, bf16[3584,3584]{1,0:T(8,128)(2,1)} %param.17, bf16[2,128,3584]{2,1,0:T(8,128)(2,1)S(1)} %copy-done.1), kind=kOutput, calls=%fused_computation.43 | convolution fusion | flops 6579421184 | bytes 31195136 | tf_op jit(solution)/shard_map/dot_general | solution.py:110
  394.2 2.5 copy.123
  396.7 1.6 copy.124
  398.3 1.6 copy.125
  399.9 17.0 %convolution_bitcast_fusion.3 = f32[256,3584]{1,0:T(8,128)} fusion(bf16[3584,28,128]{2,0,1:T(8,128)(2,1)} %param.14, bf16[256,28,64]{2,0,1:T(8,128)(2,1)} %bitcast.247, bf16[256,28,32]{2,0,1:T(8,128)(2,1)} %bitcast.246, bf16[256,28,32]{2,0,1:T(8,128)(2,1)} %bitcast.245), kind=kOutput, calls=%fused_computation.38 | convolution fusion | flops 6582173696 | bytes 31195136 | tf_op jit(solution)/shard_map/tnh,dnh->td/dot_general | solution.py:121
  417.7 3.3 convolution_bitcast_fusion.4
  422.0 1.5 fusion.120
  423.5 1.3 fusion.44
  425.2 22.9 %all-reduce = (f32[3584]{0:T(1024)}, f32[3584]{0:T(1024)}) all-reduce(f32[3584]{0:T(1024)S(1)} %get-tuple-element.71, f32[3584]{0:T(1024)S(1)} %get-tuple-element.69), channel_id=1, replica_groups=mesh['dp'=4,'cp'=8] {'cp'}, use_global_device_ids=true, to_apply=%region_16.17 | all-reduce | flops 7168 | bytes 57344 | tf_op jit(solution)/shard_map/psum | solution.py:126
  448.2 5.5 fusion.43
  453.7 2.7 copy.88
  456.4 2.7 copy.89
  459.1 166.9 %reduce-scatter.17.cloned.1.call-done = f32[448,3584]{1,0:T(8,128)} async-done(((f32[3584,3584]{1,0:T(8,128)}), f32[448,3584]{1,0:T(8,128)}) %reduce-scatter.17.cloned.1.call-update) | async-done | bytes 6422544 | tf_op jit(solution)/shard_map/reduce_scatter | solution.py:90
  626.0 253.9 %reduce-scatter.11.cloned.1.call-done = f32[448,28,128]{2,0,1:T(8,128)} async-done(((f32[3584,28,128]{2,0,1:T(8,128)}), f32[448,28,128]{2,0,1:T(8,128)}) %reduce-scatter.11.cloned.1.call-update) | async-done | bytes 6422544 | tf_op jit(solution)/shard_map/reduce_scatter | solution.py:90
  (123 shorter events, 14.7 us)
Async XLA Ops:
  7.2 4.1 copy-start.35
  7.2 73.2 %all-gather.8.cloned.1.call-start = ((), (), s32[]{:S(2)}) async-start(), calls=%async_computation.8 | async-start | bytes 4718592 | tf_op jit(solution)/shard_map/all_gather | solution.py:114
  9.1 9.3 %copy-start.32 = (f32[2,128]{1,0:T(2,128)}, f32[2,128]{1,0:T(2,128)S(1)}, u32[]{:S(2)}) copy-start(f32[2,128]{1,0:T(2,128)S(1)} %broadcast_multiply_fusion.1) | copy-start | bytes 3076
  11.3 7.1 copy-start.36
  11.3 7.1 copy-start.17
  11.3 7.1 copy-start.38
  11.3 7.1 copy-start
  11.3 7.1 copy-start.34
  18.4 2.0 copy-start.3
  20.4 4.0 copy-start.10
  20.4 2.9 copy-start.7
  21.6 3.3 copy-start.25
  24.8 164.4 %copy-start.15 = (f32[2,128,32]{1,2,0:T(8,128)}, f32[2,128,32]{1,2,0:T(8,128)S(1)}, u32[]{:S(2)}) copy-start(f32[2,128,32]{1,2,0:T(8,128)S(1)} %get-tuple-element.85) | copy-start | bytes 98308
  24.8 164.4 %copy-start.26 = (f32[2,128,32]{1,2,0:T(8,128)}, f32[2,128,32]{1,2,0:T(8,128)S(1)}, u32[]{:S(2)}) copy-start(f32[2,128,32]{1,2,0:T(8,128)S(1)} %get-tuple-element.83) | copy-start | bytes 98308
  24.9 18.2 %copy-start.19 = (bf16[2,128,4,32]{1,3,2,0:T(8,128)(2,1)}, bf16[2,128,4,32]{1,3,2,0:T(8,128)(2,1)S(1)}, u32[]{:S(2)}) copy-start(bf16[2,128,4,32]{1,3,2,0:T(8,128)(2,1)S(1)} %get-tuple-element.81) | copy-start | bytes 196612
  24.9 18.2 %copy-start.21 = (bf16[2,128,4,32]{1,3,2,0:T(8,128)(2,1)}, bf16[2,128,4,32]{1,3,2,0:T(8,128)(2,1)S(1)}, u32[]{:S(2)}) copy-start(bf16[2,128,4,32]{1,3,2,0:T(8,128)(2,1)S(1)} %get-tuple-element.82) | copy-start | bytes 196612
  25.8 162.4 %reduce-scatter.7.cloned.1.call-start = ((), (), s32[]{:S(2)}) async-start(), calls=%async_computation.9 | async-start | bytes 4718592 | tf_op jit(solution)/shard_map/reduce_scatter | solution.py:116
  47.3 5.9 copy-start.6
  152.0 72.9 %reduce-scatter.9.cloned.1.call-start = ((), (), s32[]{:S(2)}) async-start(), calls=%async_computation.10 | async-start | bytes 4718592 | tf_op jit(solution)/shard_map/reduce_scatter | solution.py:117
  168.3 1.2 copy-start.20
  168.3 1.3 copy-start.22
  168.3 22.0 %copy-start.11 = (bf16[2,128,3584]{2,1,0:T(8,128)(2,1)S(1)}, bf16[2,128,3584]{2,1,0:T(8,128)(2,1)}, u32[]{:S(2)}) copy-start(bf16[2,128,3584]{2,1,0:T(8,128)(2,1)} %copy-done.10) | copy-start | bytes 5505028
  168.4 84.1 %all-gather.6.cloned.1.call-start = ((), (), s32[]{:S(2)}) async-start(), calls=%async_computation.7 | async-start | bytes 2359296 | tf_op jit(solution)/shard_map/all_gather | solution.py:107
  170.4 108.3 %all-gather.4.cloned.1.call-start = ((), (), s32[]{:S(2)}) async-start(), calls=%async_computation.6 | async-start | bytes 2359296 | tf_op jit(solution)/shard_map/all_gather | solution.py:108
  171.4 282.4 %reduce-scatter.13.cloned.1.call-start = ((), (), s32[]{:S(2)}) async-start(), calls=%async_computation.12 | async-start | bytes 8257536 | tf_op jit(solution)/shard_map/reduce_scatter | solution.py:90
  189.2 5.2 copy-start.23
  190.3 4.1 copy-start.28
  190.3 4.1 copy-start.30
  194.5 262.0 %reduce-scatter.15.cloned.1.call-start = ((), (), s32[]{:S(2)}) async-start(), calls=%async_computation.13 | async-start | bytes 8257536 | tf_op jit(solution)/shard_map/reduce_scatter | solution.py:90
  226.0 0.7 copy-start.13
  230.8 21.7 %copy-start.9 = (bf16[2,128,4,7,128]{4,1,3,2,0:T(8,128)(2,1)S(1)}, bf16[2,128,4,7,128]{4,1,3,2,0:T(8,128)(2,1)}, u32[]{:S(2)}) copy-start(bf16[2,128,4,7,128]{4,1,3,2,0:T(8,128)(2,1)} %pad_maximum_fusion) | copy-start | bytes 5505028
  230.9 395.1 %reduce-scatter.17.cloned.1.call-start = ((), (), s32[]{:S(2)}) async-start(), calls=%async_computation.14 | async-start | bytes 57802752 | tf_op jit(solution)/shard_map/reduce_scatter | solution.py:90
  291.5 24.7 %copy-start.5 = (bf16[2,4,128,7,128]{4,2,3,1,0:T(8,128)(2,1)}, bf16[2,4,128,7,128]{4,2,3,1,0:T(8,128)(2,1)S(1)}, u32[]{:S(2)}) copy-start(bf16[2,4,128,7,128]{4,2,3,1,0:T(8,128)(2,1)S(1)} %fusion.86) | copy-start | bytes 5505028
  316.3 41.1 %copy-start.16 = (f32[2,128,32]{1,2,0:T(8,128)S(1)}, f32[2,128,32]{1,2,0:T(8,128)}, u32[]{:S(2)}) copy-start(f32[2,128,32]{1,2,0:T(8,128)} %copy-done.15) | copy-start | bytes 98308
  316.3 41.1 %copy-start.27 = (f32[2,128,32]{1,2,0:T(8,128)S(1)}, f32[2,128,32]{1,2,0:T(8,128)}, u32[]{:S(2)}) copy-start(f32[2,128,32]{1,2,0:T(8,128)} %copy-done.26) | copy-start | bytes 98308
  316.3 563.6 %reduce-scatter.11.cloned.1.call-start = ((), (), s32[]{:S(2)}) async-start(), calls=%async_computation.11 | async-start | bytes 57802752 | tf_op jit(solution)/shard_map/reduce_scatter | solution.py:90
  355.6 4.3 copy-start.12
  379.4 1.5 copy-start.1
  399.9 17.0 %copy-start.31 = (bf16[2,128,4,32]{1,3,2,0:T(8,128)(2,1)S(1)}, bf16[2,128,4,32]{1,3,2,0:T(8,128)(2,1)}, u32[]{:S(2)}) copy-start(bf16[2,128,4,32]{1,3,2,0:T(8,128)(2,1)} %copy-done.30) | copy-start | bytes 196612
  399.9 17.2 %copy-start.29 = (bf16[2,128,4,32]{1,3,2,0:T(8,128)(2,1)S(1)}, bf16[2,128,4,32]{1,3,2,0:T(8,128)(2,1)}, u32[]{:S(2)}) copy-start(bf16[2,128,4,32]{1,3,2,0:T(8,128)(2,1)} %copy-done.28) | copy-start | bytes 196612
  399.9 17.4 %copy-start.24 = (bf16[2,128,4,64]{1,3,2,0:T(8,128)(2,1)S(1)}, bf16[2,128,4,64]{1,3,2,0:T(8,128)(2,1)}, u32[]{:S(2)}) copy-start(bf16[2,128,4,64]{1,3,2,0:T(8,128)(2,1)} %copy-done.23) | copy-start | bytes 393220
  399.9 17.6 %copy-start.14 = (bf16[2,128,4,128]{1,3,2,0:T(8,128)(2,1)S(1)}, bf16[2,128,4,128]{1,3,2,0:T(8,128)(2,1)}, u32[]{:S(2)}) copy-start(bf16[2,128,4,128]{1,3,2,0:T(8,128)(2,1)} %copy-done.13) | copy-start | bytes 786436
  417.7 3.4 copy-start.4
  417.7 4.3 copy-start.8
  417.7 4.2 copy-start.18
  422.0 1.5 copy-start.33
  422.0 1.5 copy-start.37
  423.4 1.8 copy-start.2
Sparse Core Ops, SparseCore 0:
  26.0 36.3 all-gather.7
  152.1 36.0 reduce-scatter.6
  191.1 33.7 reduce-scatter.8
  226.9 25.4 all-gather.5
  254.5 24.1 all-gather.3
  280.9 44.4 reduce-scatter.12
  327.7 44.0 reduce-scatter.14
  374.8 251.1 reduce-scatter.16
  629.0 250.8 reduce-scatter.10
where the time goes:
time: 891 us; the launch traced here: 887 us
  waiting for transfers between devices  500 us (56%)
  matrix products  273 us (31%)
  local copies, waits for them, and re-layouts  49.2 us (6%)
  other arithmetic  26.3 us (3%)
  blocking collectives  22.9 us (3%)
  between operations  14.7 us (2%)
    reduce_scatter x4, waiting for transfers between devices, reduce_rows(): return lax.psum_scatter(values, 'cp', scatter_dimension=0, tiled=True)  421 us
    dot_general x1, matrix products, one_tile(): jnp.einsum('bkgql,bqkgd->blkd', grad_score, q_tile, preferred_element_typ...  39.8 us
    dot_general x1, matrix products, one_tile(): jnp.einsum('bkgql,blkd->bqkgd', grad_score, key_all, preferred_element_ty...  39.2 us
    sub x2, matrix products, tile_probs(): shifted = jnp.exp(scores - jnp.max(scores, axis=-1, keepdims=True))  33 us
    reduce_scatter x1, waiting for transfers between devices, device_step(): lax.psum_scatter(grad_v_all, 'cp', scatter_dimension=1, tiled=True)  30.4 us
    psum x1, blocking collectives, device_step(): grad_gain = lax.psum(jnp.sum(grad_h * x_hat, axis=(0, 1)), 'cp')  22.9 us
    all_gather x1, waiting for transfers between devices, device_step(): key_all = lax.all_gather(k_act, 'cp', axis=1, tiled=True)  21.5 us
    dot_general x1, matrix products, device_step(): jnp.einsum('tn,td->nd', attn_act, grad_flat, preferred_element_type=jnp.f...  21.5 us
  transfers between devices with their start and end apart: 9, of which 6 were waited for; matrix products, arithmetic and copies ran while one was open for 29% of the time, Pallas kernels for 0%

commit v1 on v0

v1 whole, which is shorter than its diff:
```python
import functools
import math
import jax
import jax.numpy as jnp
from jax import lax
from jax.experimental import pallas as pl
from jax.experimental.pallas import tpu as pltpu
from jax.sharding import PartitionSpec as P

EPS = 1e-5
ROPE_BASE = 10000.0
BF16 = jnp.bfloat16
F32 = jnp.float32
VMEM_LIMIT = 56 * 1024 * 1024
NT = (((1,), (1,)), ((), ()))


def dot(a, b):
    return jnp.dot(a, b, preferred_element_type=F32)


def dot_nt(a, b):
    return lax.dot_general(a, b, NT, preferred_element_type=F32)


def call(body, out_shape, grid, in_specs, out_specs, scratch=(), prefetch=0, flops=0, nbytes=0, name=None, aliases={}):
    return pl.pallas_call(
        body,
        out_shape=out_shape,
        grid_spec=pltpu.PrefetchScalarGridSpec(num_scalar_prefetch=prefetch, grid=grid, in_specs=in_specs, out_specs=out_specs, scratch_shapes=list(scratch)),
        compiler_params=pltpu.CompilerParams(dimension_semantics=('arbitrary',) * len(grid), vmem_limit_bytes=VMEM_LIMIT),
        cost_estimate=pl.CostEstimate(flops=int(flops), bytes_accessed=int(nbytes), transcendentals=0),
        input_output_aliases=aliases,
        name=name,
    )


def sds(shape, dtype):
    return jax.ShapeDtypeStruct(shape, dtype)


def project_body(x_ref, gain_ref, bias_ref, cos_ref, sa_ref, sb_ref, pos_ref, wq_ref, wk_ref, wv_ref, qkv_ref, ht_ref, h_ref):
    n_tok, width = x_ref.shape
    heads, head_dim = wq_ref.shape[0], wq_ref.shape[2]

    @pl.when(pl.program_id(0) == 0)
    def _():
        rows = 16

        @pl.loop(0, n_tok // rows)
        def _(step):
            sl = pl.ds(pl.multiple_of(step * rows, rows), rows)
            x = x_ref[sl, :].astype(F32)
            cen = x - jnp.mean(x, axis=-1, keepdims=True)
            inv = lax.rsqrt(jnp.mean(cen * cen, axis=-1, keepdims=True) + EPS)
            h_ref[sl, :] = ((cen * inv) * (1.0 + gain_ref[...]) + bias_ref[...]).astype(BF16)

        @pl.loop(0, width // 128)
        def _(step):
            sl = pl.ds(pl.multiple_of(step * 128, 128), 128)
            ht_ref[sl, :] = h_ref[:, sl].T

    slabs = [wq_ref[j] for j in range(heads)] + [wk_ref[0], wv_ref[0]]
    y = dot(h_ref[...], jnp.concatenate(slabs, axis=1))
    n_batch = qkv_ref.shape[1]
    seq = n_tok // n_batch
    cos, sa, sb = cos_ref[...], sa_ref[...], sb_ref[...]
    for j in range(heads + 2):
        v = y[:, j * head_dim:(j + 1) * head_dim]
        if j < heads + 1:
            v = v * cos + pltpu.roll(v, head_dim - head_dim // 4, 1) * sa + pltpu.roll(v, head_dim // 4, 1) * sb
        v = v.astype(BF16)
        for b in range(n_batch):
            qkv_ref[0, b, 0:seq, j * head_dim:(j + 1) * head_dim] = v[b * seq:(b + 1) * seq]
    for b in range(n_batch):
        qkv_ref[0, b, seq:, :] = pos_ref[b]


def project(x, gain, bias, tables, pos_rows, wq, wk, wv):
    n_batch, seq, width = x.shape
    n_tok = n_batch * seq
    kv_heads = wk.shape[0]
    group, head_dim = wq.shape[0] // kv_heads, wq.shape[2]
    cols = (group + 2) * head_dim
    pad = pos_rows.shape[1]
    whole = lambda *s: pl.BlockSpec(s, lambda i: (0,) * len(s))
    return call(
        project_body,
        (sds((kv_heads, n_batch, seq + pad, cols), BF16), sds((width, n_tok), BF16)),
        (kv_heads,),
        [whole(n_tok, width), whole(1, width), whole(1, width)] + [whole(n_tok, head_dim)] * 3 + [whole(n_batch, pad, cols),
         pl.BlockSpec((group, width, head_dim), lambda i: (i, 0, 0)),
         pl.BlockSpec((1, width, head_dim), lambda i: (i, 0, 0)),
         pl.BlockSpec((1, width, head_dim), lambda i: (i, 0, 0))],
        (pl.BlockSpec((1, n_batch, seq + pad, cols), lambda i: (i, 0, 0, 0)), whole(width, n_tok)),
        scratch=[pltpu.VMEM((n_tok, width), BF16)],
        flops=2 * n_tok * width * cols * kv_heads, nbytes=width * cols * kv_heads * 2, name='project',
    )(x.reshape(n_tok, width), gain.reshape(1, width), bias.reshape(1, width), *tables, pos_rows, wq, wk, wv)


def masked_scores(k, q, limit, tile, scale):
    s = dot_nt(k[:limit], q) * scale
    row = lax.broadcasted_iota(jnp.int32, (tile, tile), 0)
    col = lax.broadcasted_iota(jnp.int32, (tile, tile), 1)
    tail = jnp.where(row <= col, s[limit - tile:], -1e30)
    return tail if limit == tile else jnp.concatenate([s[:limit - tile], tail], axis=0)


def attend_body(tile, q_ref, k_ref, v_ref, a_ref, at_ref, stat_ref, vt_ref):
    n_seq = q_ref.shape[0] * q_ref.shape[1]
    head_dim = q_ref.shape[2]
    scale = head_dim ** -0.5
    q = q_ref[...].reshape(n_seq, head_dim)
    k = k_ref[...].reshape(n_seq, head_dim)

    @pl.when(pl.program_id(0) == 0)
    def _():
        vt_ref[...] = v_ref[...].reshape(n_seq, head_dim).T

    for t in range(n_seq // tile):
        limit = (t + 1) * tile
        sl = slice(t * tile, limit)
        s = masked_scores(k, q[sl], limit, tile, scale)
        top = jnp.max(s, axis=0, keepdims=True)
        e = jnp.exp(s - top)
        inv = 1.0 / jnp.sum(e, axis=0, keepdims=True)
        p = (e * inv).astype(BF16)
        at = dot(vt_ref[:, :limit], p).astype(BF16)
        at_ref[:, sl] = at
        a_ref[sl, :] = at.T
        stat_ref[0, 0:1, sl] = top
        stat_ref[0, 1:2, sl] = inv


def attend(qkv, seq, group, tile):
    n_src, cols = qkv.shape[0], qkv.shape[2]
    head_dim = cols // (group + 2)
    n_seq = n_src * seq
    col = lambda f: pl.BlockSpec((n_src, seq, head_dim), lambda j: (0, 0, f(j)))
    return call(
        functools.partial(attend_body, tile),
        (sds((n_seq, group * head_dim), BF16), sds((group * head_dim, n_seq), BF16), sds((group, 8, n_seq), F32)),
        (group,),
        [col(lambda j: j), col(lambda j: group), col(lambda j: group + 1)],
        (pl.BlockSpec((n_seq, head_dim), lambda j: (0, j)), pl.BlockSpec((head_dim, n_seq), lambda j: (j, 0)), pl.BlockSpec((1, 8, n_seq), lambda j: (j, 0, 0))),
        scratch=[pltpu.VMEM((head_dim, n_seq), BF16)],
        flops=4 * group * n_seq * n_seq * head_dim, nbytes=3 * n_seq * cols * 2, name='attend',
    )(qkv, qkv, qkv)


def attend_back_body(tile, q_ref, k_ref, v_ref, da_ref, stat_ref, cos_ref, sin_ref, g_ref, kt_ref, dk_ref, dv_ref):
    n_seq = q_ref.shape[0] * q_ref.shape[1]
    head_dim = q_ref.shape[2]
    quarter = head_dim // 4
    group = pl.num_programs(0) - 2
    j = pl.program_id(0)
    scale = head_dim ** -0.5

    def rotate_back(t, sl):
        cos, sin = cos_ref[:, sl], sin_ref[:, sl]
        u, w = t[:quarter], t[quarter:2 * quarter]
        return jnp.concatenate([u * cos + w * sin, w * cos - u * sin, t[2 * quarter:]], axis=0)

    @pl.when(j == 0)
    def _():
        kt_ref[...] = k_ref[...].reshape(n_seq, head_dim).T
        dk_ref[...] = jnp.zeros_like(dk_ref)
        dv_ref[...] = jnp.zeros_like(dv_ref)

    @pl.when(j < group)
    def _():
        q = q_ref[...].reshape(n_seq, head_dim)
        k = k_ref[...].reshape(n_seq, head_dim)
        v = v_ref[...].reshape(n_seq, head_dim)
        for t in range(n_seq // tile):
            limit = (t + 1) * tile
            sl = slice(t * tile, limit)
            da = da_ref[sl, :]
            s = masked_scores(k, q[sl], limit, tile, scale)
            p = jnp.exp(s - stat_ref[0, 0:1, sl]) * stat_ref[0, 1:2, sl]
            dp = dot_nt(v[:limit], da)
            row_dot = jnp.sum(p * dp, axis=0, keepdims=True)
            ds = (p * (dp - row_dot) * scale).astype(BF16)
            dv_ref[:limit, :] += dot(p.astype(BF16), da)
            dk_ref[:limit, :] += dot(ds, q[sl])
            g_ref[sl, :] = rotate_back(dot(kt_ref[:, :limit], ds), sl).T.astype(BF16)

    @pl.when(j == group)
    def _():
        g_ref[...] = rotate_back(dk_ref[...].T, slice(0, n_seq)).T.astype(BF16)

    @pl.when(j == group + 1)
    def _():
        g_ref[...] = dv_ref[...].astype(BF16)


def attend_back(qkv, da, stats, cos_t, sin_t, seq, group, tile):
    n_src, cols = qkv.shape[0], qkv.shape[2]
    head_dim = cols // (group + 2)
    n_seq = n_src * seq
    last = group - 1
    col = lambda f: pl.BlockSpec((n_src, seq, head_dim), lambda j: (0, 0, f(j)))
    cap = lambda j: jnp.minimum(j, last)
    return call(
        functools.partial(attend_back_body, tile),
        sds((n_seq, cols), BF16),
        (group + 2,),
        [col(cap), col(lambda j: group), col(lambda j: group + 1),
         pl.BlockSpec((n_seq, head_dim), lambda j: (0, cap(j))),
         pl.BlockSpec((1, 8, n_seq), lambda j: (cap(j), 0, 0)),
         pl.BlockSpec(cos_t.shape, lambda j: (0, 0)), pl.BlockSpec(sin_t.shape, lambda j: (0, 0))],
        pl.BlockSpec((n_seq, head_dim), lambda j: (0, j)),
        scratch=[pltpu.VMEM((head_dim, n_seq), BF16), pltpu.VMEM((n_seq, head_dim), F32), pltpu.VMEM((n_seq, head_dim), F32)],
        flops=10 * group * n_seq * n_seq * head_dim, nbytes=4 * n_seq * cols * 2, name='attend_back',
    )(qkv, qkv, qkv, da, stats, cos_t, sin_t)


def grad_mix_body(where_ref, dy_ref, wo_ref, da_ref):
    rows = dy_ref.shape[0] * dy_ref.shape[2]
    da_ref[...] = dot_nt(dy_ref[...].reshape(rows, dy_ref.shape[3]), wo_ref[...]).astype(BF16)


def grad_mix(where, dy_all, w_out, n_rows):
    n_dev, n_batch, seq, width = dy_all.shape
    per = 2
    return call(
        grad_mix_body,
        sds((n_dev * seq, n_rows), BF16),
        (n_dev // per,),
        [pl.BlockSpec((per, 1, seq, width), lambda i, w: (i, w[1], 0, 0)), pl.BlockSpec((n_rows, width), lambda i, w: (w[0], 0))],
        pl.BlockSpec((per * seq, n_rows), lambda i, w: (i, 0)),
        prefetch=1, flops=2 * n_dev * seq * n_rows * width, nbytes=2 * width * (n_rows + n_dev * seq), name='grad_mix',
    )(where, dy_all, w_out)


def output_body(a_ref, wo_ref, x_ref, out_ref, mix_ref):
    n_src, seq, cols = a_ref.shape
    n_batch = x_ref.shape[0]

    @pl.when(pl.program_id(0) == 0)
    def _():
        for s in range(n_src):
            mix_ref[(s % n_batch) * seq:(s % n_batch + 1) * seq, (s // n_batch) * cols:(s // n_batch + 1) * cols] = a_ref[s]

    y = dot(mix_ref[...], wo_ref[...]).reshape(x_ref.shape)
    out_ref[...] = (x_ref[...].astype(F32) + y).astype(BF16)


def output(a_recv, w_out, x, tile):
    n_batch, seq, width = x.shape
    rows = w_out.shape[0]
    return call(
        output_body,
        sds(x.shape, BF16),
        (width // tile,),
        [pl.BlockSpec(a_recv.shape, lambda i: (0, 0, 0)), pl.BlockSpec((rows, tile), lambda i: (0, i)), pl.BlockSpec((n_batch, seq, tile), lambda i: (0, 0, i))],
        pl.BlockSpec((n_batch, seq, tile), lambda i: (0, 0, i)),
        scratch=[pltpu.VMEM((n_batch * seq, rows), BF16)],
        flops=2 * n_batch * seq * rows * width, nbytes=2 * rows * width, name='output',
    )(a_recv, w_out, x)


def grad_wo_body(where_ref, own_ref, other_ref, dy_ref, out_ref, at_ref):
    n_dev, n_batch, seq, tile = dy_ref.shape

    @pl.when(pl.program_id(0) == 0)
    def _():
        mine = where_ref[1]
        for d in range(n_dev):
            src = slice(d * seq, (d + 1) * seq)
            at_ref[:, pl.ds(pl.multiple_of((d * n_batch + mine) * seq, seq), seq)] = own_ref[:, src]
            at_ref[:, pl.ds(pl.multiple_of((d * n_batch + 1 - mine) * seq, seq), seq)] = other_ref[:, src]

    out_ref[...] = dot(at_ref[...], dy_ref[...].reshape(n_dev * n_batch * seq, tile))


def grad_wo_rows(where, own, other, dy_all, tile):
    n_dev, n_batch, seq, width = dy_all.shape
    rows, n_seq = own.shape
    return call(
        grad_wo_body,
        sds((rows, width), F32),
        (width // tile,),
        [pl.BlockSpec((rows, n_seq), lambda i, w: (0, 0))] * 2 + [pl.BlockSpec((n_dev, n_batch, seq, tile), lambda i, w: (0, 0, 0, i))],
        pl.BlockSpec((rows, tile), lambda i, w: (0, i)),
        scratch=[pltpu.VMEM((rows, n_batch * n_seq), BF16)],
        prefetch=1, flops=4 * n_seq * rows * width, nbytes=4 * n_seq * width + 4 * rows * width, name='grad_wo',
    )(where, own, other, dy_all)


def grad_qkv_body(ht_ref, g_ref, dq_ref, dk_ref, dv_ref, lhs_ref):
    n_dev, rows, n_tok = ht_ref.shape
    n_batch = g_ref.shape[0]
    seq = n_tok // n_batch
    head_dim = dq_ref.shape[2]
    group = dq_ref.shape[0]

    @pl.when(pl.program_id(0) == 0)
    def _():
        for d in range(n_dev):
            for b in range(n_batch):
                lhs_ref[:, (b * n_dev + d) * seq:(b * n_dev + d + 1) * seq] = ht_ref[d, :, b * seq:(b + 1) * seq]

    g = g_ref[...].reshape(n_batch * n_dev * seq, g_ref.shape[2])
    y = dot(lhs_ref[...], g)
    for j in range(group):
        dq_ref[j] = y[:, j * head_dim:(j + 1) * head_dim]
    dk_ref[0] = y[:, group * head_dim:(group + 1) * head_dim]
    dv_ref[0] = y[:, (group + 1) * head_dim:]


def grad_qkv(ht_all, g_all, group):
    n_dev, rows, n_tok = ht_all.shape
    _, n_seq, cols = g_all.shape
    head_dim = cols // (group + 2)
    n_batch = n_tok * n_dev // n_seq
    chips = n_dev // n_batch
    return call(
        grad_qkv_body,
        (sds((chips * group, rows, head_dim), F32), sds((chips, rows, head_dim), F32), sds((chips, rows, head_dim), F32)),
        (chips,),
        [pl.BlockSpec(ht_all.shape, lambda i: (0, 0, 0)), pl.BlockSpec((n_batch, n_seq, cols), lambda i: (i, 0, 0))],
        (pl.BlockSpec((group, rows, head_dim), lambda i: (i, 0, 0)), pl.BlockSpec((1, rows, head_dim), lambda i: (i, 0, 0)), pl.BlockSpec((1, rows, head_dim), lambda i: (i, 0, 0))),
        scratch=[pltpu.VMEM((rows, n_dev * n_tok), BF16)],
        flops=2 * n_dev * n_tok * rows * cols * chips, nbytes=2 * g_all.size + 4 * rows * cols * chips, name='grad_qkv',
    )(ht_all, g_all)


def grad_x_body(where_ref, g_ref, wq_ref, wk_ref, wv_ref, x_ref, dy_ref, gain_ref, dx_ref, sums_ref, acc_ref):
    n_batch, seq, cols = g_ref.shape
    n_tok = n_batch * seq
    group = wq_ref.shape[0]
    i = pl.program_id(0)
    w = jnp.concatenate([wq_ref[j] for j in range(group)] + [wk_ref[0], wv_ref[0]], axis=1)
    part = dot_nt(g_ref[...].reshape(n_tok, cols), w)

    @pl.when(i == 0)
    def _():
        acc_ref[...] = part

    @pl.when(i > 0)
    def _():
        acc_ref[...] += part

    @pl.when(i == pl.num_programs(0) - 1)
    def _():
        rows = 16
        sums_ref[...] = jnp.zeros_like(sums_ref)

        @pl.loop(0, n_tok // rows)
        def _(step):
            sl = pl.ds(pl.multiple_of(step * rows, rows), rows)
            x = x_ref[sl, :].astype(F32)
            cen = x - jnp.mean(x, axis=-1, keepdims=True)
            inv = lax.rsqrt(jnp.mean(cen * cen, axis=-1, keepdims=True) + EPS)
            hat = cen * inv
            dh = acc_ref[sl, :]
            gh = dh * (1.0 + gain_ref[...])
            one = jnp.mean(gh, axis=-1, keepdims=True)
            two = jnp.mean(gh * hat, axis=-1, keepdims=True)
            dx_ref[sl, :] = (dy_ref[sl, :].astype(F32) + inv * (gh - one - hat * two)).astype(BF16)
            sums_ref[0] += (dh * hat)[0:8] + (dh * hat)[8:16]
            sums_ref[1] += dh[0:8] + dh[8:16]


def grad_x(where, g_all, wq, wk, wv, x, dy, gain):
    n_batch, seq, width = x.shape
    n_tok = n_batch * seq
    cols = g_all.shape[2]
    kv_heads = wk.shape[0]
    group, head_dim = wq.shape[0] // kv_heads, wq.shape[2]
    whole = lambda *s: pl.BlockSpec(s, lambda i, w: (0,) * len(s))
    return call(
        grad_x_body,
        (sds((n_tok, width), BF16), sds((2, 8, width), F32)),
        (kv_heads,),
        [pl.BlockSpec((n_batch, seq, cols), lambda i, w: (i, w[2], 0)),
         pl.BlockSpec((group, width, head_dim), lambda i, w: (i, 0, 0)), pl.BlockSpec((1, width, head_dim), lambda i, w: (i, 0, 0)), pl.BlockSpec((1, width, head_dim), lambda i, w: (i, 0, 0)),
         whole(n_tok, width), whole(n_tok, width), whole(1, width)],
        (whole(n_tok, width), whole(2, 8, width)),
        scratch=[pltpu.VMEM((n_tok, width), F32)],
        prefetch=1, flops=2 * n_tok * width * cols * kv_heads, nbytes=2 * width * cols * kv_heads, name='grad_x',
    )(where, g_all, wq, wk, wv, x.reshape(n_tok, width), dy.reshape(n_tok, width), gain.reshape(1, width))


def solution(mesh):
    n_dev = mesh.shape['cp']

    def device_step(x_act, d_out, positions, ln_gain, ln_bias, w_query, w_key, w_value, w_out):
        n_batch, seq, width = x_act.shape
        q_heads, (kv_heads, head_dim) = w_query.shape[1], w_key.shape[1:]
        group = q_heads // kv_heads
        quarter = head_dim // 4
        chips = n_dev // n_batch
        assert chips == kv_heads and q_heads * head_dim == width
        me = lax.axis_index('cp')
        where = jnp.stack([me // n_batch, me % n_batch, me]).astype(jnp.int32)
        swap = [(i, i ^ 1) for i in range(n_dev)]

        dy_all = lax.all_gather(d_out, 'cp', axis=0)
        freq = jnp.exp(jnp.arange(quarter, dtype=F32) * (-2.0 * math.log(ROPE_BASE) / (head_dim // 2)))
        angles = positions.astype(F32).reshape(n_batch * seq, 1) * freq
        cos, sin = jnp.cos(angles), jnp.sin(angles)
        rest = jnp.zeros((n_batch * seq, head_dim - 2 * quarter), F32)
        none = jnp.zeros_like(sin)
        tables = (jnp.concatenate([cos, cos, rest + 1.0], axis=1), jnp.concatenate([-sin, none, rest], axis=1), jnp.concatenate([none, sin, rest], axis=1))
        cols = (group + 2) * head_dim
        pair = jnp.stack([positions // 256, positions % 256], axis=1).astype(BF16).reshape(n_batch, 1, 2 * seq)
        pos_rows = jnp.pad(pair, ((0, 0), (0, 7), (0, cols - 2 * seq)))
        wq = jnp.transpose(w_query, (1, 0, 2))
        wk = jnp.transpose(w_key, (1, 0, 2))
        wv = jnp.transpose(w_value, (1, 0, 2))

        qkv_send, ht = project(x_act, ln_gain, ln_bias, tables, pos_rows, wq, wk, wv)
        qkv = lax.all_to_all(qkv_send.reshape(n_dev, seq + 8, cols), 'cp', 0, 0, tiled=True)
        ht_all = lax.all_to_all(ht.reshape(n_dev, width // n_dev, n_batch * seq), 'cp', 0, 0, tiled=True)
        spots = qkv[:, seq, :2 * seq].astype(F32).reshape(n_dev, 2, seq)
        spots = (spots[:, 0] * 256.0 + spots[:, 1]).reshape(1, n_dev * seq)
        angles_t = freq[:, None] * spots
        cos_t, sin_t = jnp.cos(angles_t), jnp.sin(angles_t)

        attn, attn_t, stats = attend(qkv, seq, group, 256)
        a_recv = lax.all_to_all(attn.reshape(n_dev, seq, group * head_dim), 'cp', 0, 0, tiled=True)
        half = width // n_dev
        attn_t = attn_t.reshape(n_batch, half, n_dev * seq)
        at_own = lax.dynamic_index_in_dim(attn_t, where[1], 0, keepdims=False)
        at_other = lax.ppermute(lax.dynamic_index_in_dim(attn_t, 1 - where[1], 0, keepdims=False), 'cp', swap)
        da = grad_mix(where, dy_all, w_out, group * head_dim)
        g_own = attend_back(qkv, da, stats, cos_t, sin_t, seq, group, 256)
        g_all = lax.all_gather(g_own, 'cp', axis=0)
        block_out = output(a_recv, w_out, x_act, 512)
        grad_wo = grad_wo_rows(where, at_own, at_other, dy_all, 512)
        dx, sums = grad_x(where, g_all, wq, wk, wv, x_act, d_out, ln_gain)
        gq, gk, gv = grad_qkv(ht_all, g_all, group)
        total = jnp.sum(sums, axis=1)
        total = total + lax.ppermute(total, 'cp', swap)
        total = total + lax.ppermute(total, 'cp', [(i, (i // 2 ^ 1) * 2 + i % 2) for i in range(n_dev)])
        total = total + lax.ppermute(total, 'cp', [(i, (i // 2 ^ 3) * 2 + i % 2) for i in range(n_dev)])
        rows = lambda t: jnp.transpose(t, (1, 0, 2))
        return (block_out, dx.reshape(x_act.shape), rows(gq), rows(gk), rows(gv), grad_wo, total[0], total[1])

    return jax.shard_map(device_step, mesh=mesh, in_specs=(P('dp', 'cp', None), P('dp', 'cp', None), P('dp', 'cp'), P(None), P(None), P(None, None, None), P(None, None, None), P(None, None, None), P(None, None)), out_specs=(P('dp', 'cp', None), P('dp', 'cp', None), P(('dp', 'cp'), None, None), P(('dp', 'cp'), None, None), P(('dp', 'cp'), None, None), P(('dp', 'cp'), None), P('dp'), P('dp')), check_vma=False)
```

time: 891 us -> 373 us (0.42)
  waiting for transfers between devices: 500 us -> 170 us
  matrix products: 273 us -> 0 us
  Pallas kernels: 0 us -> 144 us
  local copies, waits for them, and re-layouts: 49.2 us -> 19.2 us
  blocking collectives: 22.9 us -> 0 us
  other arithmetic: 26.3 us -> 5.45 us
  starting transfers between devices: 1.11 us -> 19.1 us
    reduce_scatter x6 -> x0, waiting for transfers between devices: 468 us -> none  [the longest x4 421 us: reduce_rows(): return lax.psum_scatter(values, 'cp', scatter_dimension=0, tiled=True)]
    dot_general x17 -> x0, matrix products: 240 us -> none  [the longest x1 39.8 us: one_tile(): jnp.einsum('bkgql,bqkgd->blkd', grad_score, q_tile, preferred_element_typ...]
    pallas_call x0 -> x8, Pallas kernels: none -> 144 us  [the longest x1 25.1 us: grad_x(): call(grad_x_body, (sds((n_tok, width), BF16), sds((2, 8, width), F32)), (...]
    all_to_all x0 -> x3, waiting for transfers between devices: none -> 89.6 us  [the longest x1 57 us: device_step(): lax.all_to_all(qkv_send.reshape(n_dev, seq + 8, cols), 'cp', 0, 0, tiled=...]
    all_gather x3 -> x2, waiting for transfers between devices: 31.3 us -> 79.3 us  [the longest x1 79.3 us: device_step(): g_all = lax.all_gather(g_own, 'cp', axis=0)]
    sub x2 -> x0, matrix products: 33 us -> none  [tile_probs(): shifted = jnp.exp(scores - jnp.max(scores, axis=-1, keepdims=True))]
    psum x1 -> x0, blocking collectives: 22.9 us -> none  [device_step(): grad_gain = lax.psum(jnp.sum(grad_h * x_hat, axis=(0, 1)), 'cp')]
    all_to_all x0 -> x3, starting transfers between devices: none -> 16.8 us  [the longest x1 6.27 us: device_step(): lax.all_to_all(ht.reshape(n_dev, width // n_dev, n_batch * seq), 'cp', 0,...]
  transfers between devices with their start and end apart: 9 -> 9, of which waited for: 6 -> 3; matrix products, arithmetic and copies ran while one was open for 29% -> 6% of each run, Pallas kernels for 0% -> 30%
where the time goes in v1:
time: 373 us; the launch traced here: 372 us
  waiting for transfers between devices  170 us (46%)
  Pallas kernels  144 us (39%)
  local copies, waits for them, and re-layouts  19.2 us (5%)
  starting transfers between devices  19.1 us (5%)
  between operations  14.2 us (4%)
  other arithmetic  5.45 us (1%)
    all_gather x1, waiting for transfers between devices, device_step(): g_all = lax.all_gather(g_own, 'cp', axis=0)  79.3 us
    all_to_all x1, waiting for transfers between devices, device_step(): lax.all_to_all(qkv_send.reshape(n_dev, seq + 8, cols), 'cp', 0, 0, tiled=...  57 us
    all_to_all x1, waiting for transfers between devices, device_step(): lax.all_to_all(attn.reshape(n_dev, seq, group * head_dim), 'cp', 0, 0, ti...  32.6 us
    pallas_call x1, Pallas kernels, grad_x(): call(grad_x_body, (sds((n_tok, width), BF16), sds((2, 8, width), F32)), (...  25.1 us
    pallas_call x1, Pallas kernels, project(): call(project_body, (sds((kv_heads, n_batch, seq + pad, cols), BF16), sds(...  22.6 us
    pallas_call x1, Pallas kernels, attend_back(): call(functools.partial(attend_back_body, tile), sds((n_seq, cols), BF16),...  20.8 us
    pallas_call x1, Pallas kernels, attend(): call(functools.partial(attend_body, tile), (sds((n_seq, group * head_dim)...  17.4 us
    pallas_call x1, Pallas kernels, grad_qkv(): call(grad_qkv_body, (sds((chips * group, rows, head_dim), F32), sds((chip...  15.6 us
  transfers between devices with their start and end apart: 9, of which 3 were waited for; matrix products, arithmetic and copies ran while one was open for 6% of the time, Pallas kernels for 30%

profile of v1, /device:TPU:81, one launch (start us, length us, event | category | flops | bytes accessed | tf_op | source)
XLA Modules:
  0.0 371.7 jit_solution(1356329263072134828)
XLA Ops:
  7.2 0.1 all-gather.5.cloned.1.call-start
  7.2 0.7 all-gather.5.cloned.1.call-update
  8.0 0.1 pad.15.clone
  8.1 0.1 pad.18.clone
  8.1 0.8 fusion.4
  8.9 1.3 reshape.88.gain_ref
  10.3 1.3 reshape.89.bias_ref
  11.6 0.6 pad.4.pos_ref
  12.2 0.5 multiply_sine_fusion.1
  12.8 0.9 maximum_maximum_fusion.2
  13.7 7.1 %copy_bitcast_fusion = (bf16[4,3584,128]{2,1,0:T(8,128)(2,1)}, bf16[4,3584,128]{2,1,0:T(8,128)(2,1)}) fusion(bf16[3584,4,128]{2,1,0:T(4,128)(2,1)} %param.16, bf16[3584,4,128]{2,1,0:T(4,128)(2,1)} %param.15), kind=kLoop, calls=%fused_computation | loop fusion | bytes 14680064 | tf_op jit(solution)/shard_map/transpose | solution.py:412
  20.8 22.6 %project.1 = (bf16[4,2,136,1152]{3,2,1,0:T(8,128)(2,1)}, bf16[3584,256]{1,0:T(8,128)(2,1)}) custom-call(bf16[256,3584]{1,0:T(8,128)(2,1)} %bitcast.38, f32[1,3584]{1,0:T(1,128)} %reshape.88.gain_ref, f32[1,3584]{1,0:T(1,128)} %reshape.89.bias_ref, f32[256,128]{1,0:T(8,128)} %get-tuple-element.66.cos_ref, f32[256,128]{1,0:T(8,128)} %get-tuple-element.57.sa_ref, ...), custom_call_target="tpu_custom_call" | custom-call | flops 8455716864 | bytes 33030144 | tf_op jit(solution)/shard_map/project/pallas_call | solution.py:87
  43.5 6.0 %all-to-all-start = ((bf16[8,136,1152]{2,1,0:T(8,128)(2,1)}), bf16[8,136,1152]{2,1,0:T(8,128)(2,1)S(1)}, u32[]{:S(2)}, u32[]{:S(2)}) async-start(bf16[8,136,1152]{2,1,0:T(8,128)(2,1)} %bitcast.43), calls=%async_computation | async-start | bytes 5013504 | tf_op jit(solution)/shard_map/all_to_all | solution.py:415
  49.5 0.0 all-gather.7.cloned.1.call-start
  49.5 0.7 pad_add_fusion.where_ref
  50.2 57.0 %all-to-all-done.q_ref.k_ref.v_ref = bf16[8,136,1152]{2,1,0:T(8,128)(2,1)S(1)} async-done(((bf16[8,136,1152]{2,1,0:T(8,128)(2,1)}), bf16[8,136,1152]{2,1,0:T(8,128)(2,1)S(1)}, u32[]{:S(2)}, u32[]{:S(2)}) %all-to-all-start) | async-done | bytes 2506784 | tf_op jit(solution)/shard_map/all_to_all | solution.py:415
  107.1 0.0 copy-start.1
  107.1 1.5 multiply_sine_fusion
  108.6 0.0 copy-done.1
  108.6 17.4 %attend.1 = (bf16[1024,896]{1,0:T(8,128)(2,1)}, bf16[896,1024]{1,0:T(8,128)(2,1)}, f32[7,8,1024]{2,1,0:T(8,128)}) custom-call(bf16[8,136,1152]{2,1,0:T(8,128)(2,1)} %copy-done.1, bf16[8,136,1152]{2,1,0:T(8,128)(2,1)} %copy-done.1, bf16[8,136,1152]{2,1,0:T(8,128)(2,1)} %copy-done.1), custom_call_target="tpu_custom_call" | custom-call | flops 3758096384 | bytes 7077888 | tf_op jit(solution)/shard_map/attend/pallas_call | solution.py:140
  126.1 0.0 all-gather.5.cloned.1.call-done
  126.1 13.3 %grad_mix.1.da_ref = bf16[1024,896]{1,0:T(8,128)(2,1)} custom-call(s32[3]{0:T(128)} %pad_add_fusion.where_ref, bf16[8,2,128,3584]{3,2,1,0:T(8,128)(2,1)} %bitcast.40, bf16[3584,3584]{1,0:T(8,128)(2,1)} %wo_ref.3), custom_call_target="tpu_custom_call" | custom-call | flops 6576668672 | bytes 13762560 | tf_op jit(solution)/shard_map/grad_mix/pallas_call | solution.py:226
  139.4 20.8 %attend_back.1 = bf16[1024,1152]{1,0:T(8,128)(2,1)} custom-call(bf16[8,136,1152]{2,1,0:T(8,128)(2,1)} %copy-done.1, bf16[8,136,1152]{2,1,0:T(8,128)(2,1)} %copy-done.1, bf16[8,136,1152]{2,1,0:T(8,128)(2,1)} %copy-done.1, bf16[1024,896]{1,0:T(8,128)(2,1)} %grad_mix.1.da_ref, f32[7,8,1024]{2,1,0:T(8,128)} %get-tuple-element.20.stat_ref, ...), custom_call_target="tpu_custom_call" | custom-call | flops 9395240960 | bytes 9437184 | tf_op jit(solution)/shard_map/attend_back/pallas_call | solution.py:204
  160.2 0.1 all-gather.7.cloned.1.call-update
  160.2 4.5 %all-to-all-start.1 = ((bf16[8,128,896]{2,1,0:T(8,128)(2,1)}), bf16[8,128,896]{2,1,0:T(8,128)(2,1)S(1)}, u32[]{:S(2)}, u32[]{:S(2)}) async-start(bf16[8,128,896]{2,1,0:T(8,128)(2,1)} %bitcast.45), calls=%async_computation.1 | async-start | bytes 3670016 | tf_op jit(solution)/shard_map/all_to_all | solution.py:423
  164.7 2.5 dynamic-slice_bitcast_fusion
  167.2 0.5 collective-permute-start
  167.7 32.6 %all-to-all-done.1.a_ref = bf16[8,128,896]{2,1,0:T(8,128)(2,1)S(1)} async-done(((bf16[8,128,896]{2,1,0:T(8,128)(2,1)}), bf16[8,128,896]{2,1,0:T(8,128)(2,1)S(1)}, u32[]{:S(2)}, u32[]{:S(2)}) %all-to-all-start.1) | async-done | bytes 1835040 | tf_op jit(solution)/shard_map/all_to_all | solution.py:423
  200.3 0.0 copy-start
  200.3 6.3 %all-to-all-start.2 = ((bf16[8,448,256]{2,1,0:T(8,128)(2,1)}), bf16[8,448,256]{2,1,0:T(8,128)(2,1)}, u32[]{:S(2)}, u32[]{:S(2)}) async-start(bf16[8,448,256]{2,1,0:T(8,128)(2,1)} %bitcast.44), calls=%async_computation.2 | async-start | bytes 3670016 | tf_op jit(solution)/shard_map/all_to_all | solution.py:416
  206.6 79.3 %all-gather.7.cloned.1.call-done = bf16[8192,1152]{1,0:T(8,128)(2,1)} async-done(((bf16[1024,1152]{1,0:T(8,128)(2,1)}), bf16[8192,1152]{1,0:T(8,128)(2,1)}) %all-gather.7.cloned.1.call-update) | async-done | bytes 18874384 | tf_op jit(solution)/shard_map/all_gather | solution.py:430
  285.9 25.1 %grad_x.1 = (bf16[256,3584]{1,0:T(8,128)(2,1)}, f32[2,8,3584]{2,1,0:T(8,128)}) custom-call(s32[3]{0:T(128)} %pad_add_fusion.where_ref, bf16[8,1024,1152]{2,1,0:T(8,128)(2,1)} %bitcast.36, bf16[28,3584,128]{2,1,0:T(8,128)(2,1)} %bitcast.35, bf16[4,3584,128]{2,1,0:T(8,128)(2,1)} %get-tuple-element.68.wk_ref, bf16[4,3584,128]{2,1,0:T(8,128)(2,1)} %get-tuple-element.67.wv_ref, ...), custom_call_target="tpu_custom_call" | custom-call | flops 8455716864 | bytes 33030144 | tf_op jit(solution)/shard_map/grad_x/pallas_call | solution.py:373
  310.9 0.0 copy-done
  310.9 1.0 reduce_sum.9
  312.0 0.4 collective-permute-start.1
  312.3 14.8 %output.1 = bf16[2,128,3584]{2,1,0:T(8,128)(2,1)} custom-call(bf16[8,128,896]{2,1,0:T(8,128)(2,1)} %copy-done, bf16[3584,3584]{1,0:T(8,128)(2,1)} %wo_ref.3, bf16[2,128,3584]{2,1,0:T(8,128)(2,1)} %x_ref.1), custom_call_target="tpu_custom_call" | custom-call | flops 6576668672 | bytes 25690112 | tf_op jit(solution)/shard_map/output/pallas_call | solution.py:252
  327.1 0.0 collective-permute-done.1
  327.1 0.1 collective-permute-start.2
  327.3 0.0 collective-permute-done.other_ref
  327.3 14.6 %grad_wo.1 = f32[448,3584]{1,0:T(8,128)} custom-call(s32[3]{0:T(128)} %pad_add_fusion.where_ref, bf16[448,1024]{1,0:T(8,128)(2,1)} %get-tuple-element.55.own_ref, bf16[448,1024]{1,0:T(8,128)(2,1)} %collective-permute-done.other_ref, bf16[8,2,128,3584]{3,2,1,0:T(8,128)(2,1)} %bitcast.41), custom_call_target="tpu_custom_call" | custom-call | flops 6576668672 | bytes 21102592 | tf_op jit(solution)/shard_map/grad_wo/pallas_call | solution.py:280
  341.8 0.0 collective-permute-done.2
  341.8 1.3 collective-permute-start.3
  343.2 0.0 all-to-all-done.2.ht_ref
  343.2 15.6 %grad_qkv.1 = (f32[28,448,128]{2,1,0:T(8,128)}, f32[4,448,128]{2,1,0:T(8,128)}, f32[4,448,128]{2,1,0:T(8,128)}) custom-call(bf16[8,448,256]{2,1,0:T(8,128)(2,1)} %all-to-all-done.2.ht_ref, bf16[8,1024,1152]{2,1,0:T(8,128)(2,1)} %bitcast.37), custom_call_target="tpu_custom_call" | custom-call | flops 8455716864 | bytes 27131904 | tf_op jit(solution)/shard_map/grad_qkv/pallas_call | solution.py:318
  358.8 2.7 copy.30
  361.5 2.7 copy.31
  364.2 0.0 collective-permute-done.3
  364.2 0.7 slice_reduce_fusion
  (11 shorter events, 0.1 us)
Async XLA Ops:
  7.2 118.9 %all-gather.5.cloned.1.call-start = ((), (), s32[]{:S(2)}) async-start(), calls=%async_computation.3 | async-start | bytes 16515072 | tf_op jit(solution)/shard_map/all_gather | solution.py:400
  43.5 63.6 %all-to-all-start = ((bf16[8,136,1152]{2,1,0:T(8,128)(2,1)}), bf16[8,136,1152]{2,1,0:T(8,128)(2,1)S(1)}, u32[]{:S(2)}, u32[]{:S(2)}) async-start(bf16[8,136,1152]{2,1,0:T(8,128)(2,1)} %bitcast.43), calls=%async_computation | async-start | bytes 5013504 | tf_op jit(solution)/shard_map/all_to_all | solution.py:415
  49.5 236.4 %all-gather.7.cloned.1.call-start = ((), (), s32[]{:S(2)}) async-start(), calls=%async_computation.4 | async-start | bytes 21233664 | tf_op jit(solution)/shard_map/all_gather | solution.py:430
  107.1 1.5 copy-start.1
  160.2 40.1 %all-to-all-start.1 = ((bf16[8,128,896]{2,1,0:T(8,128)(2,1)}), bf16[8,128,896]{2,1,0:T(8,128)(2,1)S(1)}, u32[]{:S(2)}, u32[]{:S(2)}) async-start(bf16[8,128,896]{2,1,0:T(8,128)(2,1)} %bitcast.45), calls=%async_computation.1 | async-start | bytes 3670016 | tf_op jit(solution)/shard_map/all_to_all | solution.py:423
  167.2 160.0 %collective-permute-start = (bf16[448,1024]{1,0:T(8,128)(2,1)S(1)}, bf16[448,1024]{1,0:T(8,128)(2,1)}, u32[]{:S(2)}, u32[]{:S(2)}) collective-permute-start(bf16[448,1024]{1,0:T(8,128)(2,1)S(1)} %get-tuple-element.54), channel_id=1, source_target_pairs={{0,1},{1,0},{2,3},{3,2},{4,5},{5,4},{6,7},{7,6},{8,9},{9,8},{10,11... | collective-permute-start | bytes 2752520 | tf_op jit(solution)/shard_map/ppermute | solution.py:427
  200.3 110.6 %copy-start = (bf16[8,128,896]{2,1,0:T(8,128)(2,1)}, bf16[8,128,896]{2,1,0:T(8,128)(2,1)S(1)}, u32[]{:S(2)}) copy-start(bf16[8,128,896]{2,1,0:T(8,128)(2,1)S(1)} %all-to-all-done.1.a_ref) | copy-start | bytes 5505028
  200.3 142.8 %all-to-all-start.2 = ((bf16[8,448,256]{2,1,0:T(8,128)(2,1)}), bf16[8,448,256]{2,1,0:T(8,128)(2,1)}, u32[]{:S(2)}, u32[]{:S(2)}) async-start(bf16[8,448,256]{2,1,0:T(8,128)(2,1)} %bitcast.44), calls=%async_computation.2 | async-start | bytes 3670016 | tf_op jit(solution)/shard_map/all_to_all | solution.py:416
  312.0 15.1 %collective-permute-start.1 = (f32[2,3584]{1,0:T(2,128)S(1)}, f32[2,3584]{1,0:T(2,128)S(1)}, u32[]{:S(2)}, u32[]{:S(2)}) collective-permute-start(f32[2,3584]{1,0:T(2,128)S(1)} %reduce_sum.9), channel_id=1, source_target_pairs={{0,1},{1,0},{2,3},{3,2},{4,5},{5,4},{6,7},{7,6},{8,9},{9,8},{10,11... | collective-permute-start | bytes 86024 | tf_op jit(solution)/shard_map/ppermute | solution.py:436
  327.1 14.7 %collective-permute-start.2 = (f32[2,3584]{1,0:T(2,128)S(1)}, f32[2,3584]{1,0:T(2,128)S(1)}, u32[]{:S(2)}, u32[]{:S(2)}) collective-permute-start(f32[2,3584]{1,0:T(2,128)S(1)} %add.51), channel_id=1, source_target_pairs={{0,2},{1,3},{2,0},{3,1},{4,6},{5,7},{6,4},{7,5},{8,10},{9,11},{10,... | collective-permute-start | bytes 86024 | tf_op jit(solution)/shard_map/ppermute | solution.py:437
  341.8 22.4 %collective-permute-start.3 = (f32[2,3584]{1,0:T(2,128)S(1)}, f32[2,3584]{1,0:T(2,128)S(1)}, u32[]{:S(2)}, u32[]{:S(2)}) collective-permute-start(f32[2,3584]{1,0:T(2,128)S(1)} %add.52), channel_id=1, source_target_pairs={{0,6},{1,7},{2,4},{3,5},{4,2},{5,3},{6,0},{7,1},{8,14},{9,15},{10,... | collective-permute-start | bytes 86024 | tf_op jit(solution)/shard_map/ppermute | solution.py:438
Sparse Core Ops, SparseCore 0:
  9.6 104.5 all-gather.4
  160.3 125.4 all-gather.6

commit v2 on v0

v2 whole, which is shorter than its diff:
```python
import functools
import math
import jax
import jax.numpy as jnp
from jax import lax
from jax.experimental import pallas as pl
from jax.experimental.pallas import tpu as pltpu
from jax.sharding import PartitionSpec as P

EPS = 1e-5
ROPE_BASE = 10000.0
BF16 = jnp.bfloat16
F32 = jnp.float32
VMEM_LIMIT = 63 * 1024 * 1024
NT = (((1,), (1,)), ((), ()))
ANY = pl.BlockSpec(memory_space=pl.ANY)
VM = pl.BlockSpec(memory_space=pltpu.VMEM)
CORES = 2
PAD = 8
ATTN_TILE = 256
COL_TILE = 512
ROWS = 16


def dot(a, b):
    return jnp.dot(a, b, preferred_element_type=F32)


def dot_nt(a, b):
    return lax.dot_general(a, b, NT, preferred_element_type=F32)


def sds(shape, dtype):
    return jax.ShapeDtypeStruct(shape, dtype)


def block(i, size):
    return pl.ds(pl.multiple_of(i * size, size), size)


class Place:
    def __init__(self, n_dev):
        self.n_dev = n_dev
        self.chips = n_dev // CORES
        self.me = lax.axis_index('cp')
        self.chip = self.me // CORES
        self.core = self.me % CORES
        self.partner = self.chip * CORES + 1 - self.core

    def ring(self, step):
        return lax.rem(self.chip + self.chips + step, self.chips)

    def dev(self, step, core):
        return self.ring(step) * CORES + core

    def peers(self, far):
        near = [self.partner] + [self.dev(s, c) for s in (1, -1) for c in range(CORES)]
        return near + ([self.dev(2, c) for c in range(CORES)] if far else [])


def send(src, dst, ssem, rsem, to):
    return pltpu.make_async_remote_copy(src_ref=src, dst_ref=dst, send_sem=ssem, recv_sem=rsem, device_id={'cp': to}, device_id_type=pl.DeviceIdType.MESH)


def meet(peers):
    barrier = pltpu.get_barrier_semaphore()
    for peer in peers:
        pl.semaphore_signal(barrier, inc=1, device_id={'cp': peer}, device_id_type=pl.DeviceIdType.MESH)
    pl.semaphore_wait(barrier, len(peers))


class Exchange:
    def __init__(self, at, src, dst, relay, ssem, rsem):
        self.at, self.src, self.dst, self.relay, self.ssem, self.rsem = at, src, dst, relay, ssem, rsem
        near = [(0, 1 - at.core)] + [(s, c) for s in (1, -1) for c in range(CORES)]
        n = at.n_dev
        self.near = [send(src(at.dev(s, c)), dst(at.me), ssem.at[i], rsem.at[at.me], at.dev(s, c)) for i, (s, c) in enumerate(near)]
        self.far = [send(src(at.dev(2, i)), relay.at[i], ssem.at[5 + i], rsem.at[n + i], at.dev(step, at.core)) for i, step in enumerate((1, -1))]
        self.on = [send(relay.at[i], dst(at.dev(-step, at.core)), ssem.at[7 + i], rsem.at[at.dev(-step, at.core)], at.dev(step, i)) for i, step in enumerate((1, -1))]

    def start(self):
        for copy in self.far + self.near:
            copy.start()

    def pass_on(self):
        for far, on in zip(self.far, self.on):
            far.wait_recv()
            on.start()

    def wait_recv(self):
        at = self.at
        for j in range(1, at.n_dev):
            origin = lax.rem(at.me + j, at.n_dev)
            send(self.src(at.me), self.dst(origin), self.ssem.at[0], self.rsem.at[origin], at.partner).wait_recv()

    def wait_send(self):
        for copy in self.far + self.near + self.on:
            copy.wait_send()


def layer_norm(x, gain, bias=None):
    cen = x - jnp.mean(x, axis=-1, keepdims=True)
    inv = lax.rsqrt(jnp.mean(cen * cen, axis=-1, keepdims=True) + EPS)
    return cen * inv, inv


def masked_scores(k, q, limit, tile, scale):
    s = dot_nt(k[:limit], q) * scale
    row = lax.broadcasted_iota(jnp.int32, (tile, tile), 0)
    col = lax.broadcasted_iota(jnp.int32, (tile, tile), 1)
    tail = jnp.where(row <= col, s[limit - tile:], -1e30)
    return tail if limit == tile else jnp.concatenate([s[:limit - tile], tail], axis=0)


def front_body(n_dev, group, x_ref, gain_ref, bias_ref, cos_ref, sa_ref, sb_ref, pos_ref, freq_ref, dy_ref, wq_ref, wk_ref, wv_ref, wo_ref,
               dy_all, ht_all, a_all, g_out, dwo_out,
               h_ref, ht_ref, dyo_ref, qs_ref, qkv_ref, a_ref, at_ref, at2_ref, stat_ref, da_ref, g_ref, kt_ref, vt_ref, dk_ref, dv_ref,
               cost_ref, sint_ref, relay_q, relay_h, relay_a,
               dy_ssem, dy_rsem, q_ssem, q_rsem, h_ssem, h_rsem, a_ssem, a_rsem, t_sem, loc_sem, mix_sem):
    at = Place(n_dev)
    n_batch, seq, width = dy_ref.shape
    n_tok = n_batch * seq
    head_dim = wq_ref.shape[2]
    cols = (group + 2) * head_dim
    n_rows = group * head_dim
    half = n_rows // CORES
    n_seq = n_dev * seq
    quarter = head_dim // 4
    scale = head_dim ** -0.5
    core, me = at.core, at.me

    meet(at.peers(False))

    sub = seq // 2
    first = [send(dy_ref.at[b], dy_all.at[me, b], dy_ssem.at[b], dy_rsem.at[b], at.dev(step, core)) for b, step in enumerate((1, -1))]
    second = [[send(dy_ref.at[1 - b, pl.ds(p * sub, sub)], dy_all.at[me, 1 - b, pl.ds(p * sub, sub)], dy_ssem.at[2 + 2 * b + p], dy_rsem.at[2 + 2 * b + p], at.dev(step, core)) for p in range(2)] for b, step in enumerate((1, -1))]
    origin = [at.dev(-1, core), at.dev(1, core)]
    far_dev = at.dev(2, core)
    again = [send(dy_all.at[origin[b], b], dy_all.at[origin[b], b], dy_ssem.at[6 + b], dy_rsem.at[6 + b], at.dev(step, core)) for b, step in enumerate((1, -1))]
    own_across = send(dy_ref, dy_all.at[me], dy_ssem.at[8], dy_rsem.at[8], at.partner)
    first_across = [send(dy_all.at[origin[b], b], dy_all.at[origin[b], b], dy_ssem.at[9 + b], dy_rsem.at[9 + b], at.partner) for b in range(2)]
    second_across = [send(dy_all.at[origin[b], 1 - b], dy_all.at[origin[b], 1 - b], dy_ssem.at[11 + b], dy_rsem.at[11 + b], at.partner) for b in range(2)]
    far_across = [send(dy_all.at[far_dev, b], dy_all.at[far_dev, b], dy_ssem.at[13 + b], dy_rsem.at[13 + b], at.partner) for b in range(2)]
    for b in range(2):
        first[b].start()
        second[b][0].start()
    own_across.start()
    dy_in = pltpu.make_async_copy(dy_ref, dyo_ref, loc_sem.at[0])
    dy_in.start()

    @pl.loop(0, n_tok // ROWS)
    def _(step):
        sl = block(step, ROWS)
        hat, _ = layer_norm(x_ref[sl, :].astype(F32), None)
        h_ref[sl, :] = (hat * (1.0 + gain_ref[...]) + bias_ref[...]).astype(BF16)

    def project(wq, wk, wv):
        chip = pl.program_id(0)
        slabs = [wq[j] for j in range(group)] + [wk[0], wv[0]]
        y = dot(h_ref[...], jnp.concatenate(slabs, axis=1))
        cos, sa, sb = cos_ref[...], sa_ref[...], sb_ref[...]
        for j in range(group + 2):
            v = y[:, j * head_dim:(j + 1) * head_dim]
            if j < group + 1:
                v = v * cos + pltpu.roll(v, head_dim - quarter, 1) * sa + pltpu.roll(v, quarter, 1) * sb
            v = v.astype(BF16)
            for b in range(n_batch):
                qs_ref[chip * n_batch + b, 0:seq, j * head_dim:(j + 1) * head_dim] = v[b * seq:(b + 1) * seq]
        for b in range(n_batch):
            qs_ref[chip * n_batch + b, seq:, :] = pos_ref[b]

    pltpu.emit_pipeline(
        project,
        grid=(at.chips,),
        in_specs=[pl.BlockSpec((group, width, head_dim), lambda i: (i, 0, 0)), pl.BlockSpec((1, width, head_dim), lambda i: (i, 0, 0)), pl.BlockSpec((1, width, head_dim), lambda i: (i, 0, 0))],
        out_specs=[],
    )(wq_ref, wk_ref, wv_ref)

    qkv = Exchange(at, lambda d: qs_ref.at[d], lambda d: qkv_ref.at[d], relay_q, q_ssem, q_rsem)
    qkv.start()
    dy_in.wait()
    dy_keep = pltpu.make_async_copy(dyo_ref, dy_all.at[me], loc_sem.at[0])
    dy_keep.start()
    qkv_ref[me] = qs_ref[me]

    @pl.loop(0, width // 128)
    def _(step):
        sl = block(step, 128)
        ht_ref[sl, :] = h_ref[:, sl].T

    qkv.pass_on()
    for b in range(2):
        second[b][1].start()
    for b in range(2):
        first[b].wait_recv()
        again[b].start()
        first_across[b].start()
    hcols = Exchange(at, lambda d: ht_ref.at[block(d, half)], lambda d: ht_all.at[d], relay_h, h_ssem, h_rsem)
    hcols.start()
    h_keep = pltpu.make_async_copy(ht_ref.at[block(me, half)], ht_all.at[me], loc_sem.at[1])
    h_keep.start()

    qkv.wait_recv()
    k_all = lambda: qkv_ref[:, 0:seq, n_rows:n_rows + head_dim].reshape(n_seq, head_dim)
    v_all = lambda: qkv_ref[:, 0:seq, n_rows + head_dim:].reshape(n_seq, head_dim)
    q_head = lambda j: qkv_ref[:, 0:seq, block(j, head_dim)].reshape(n_seq, head_dim)
    kt_ref[...] = k_all().T
    vt_ref[...] = v_all().T

    @pl.loop(0, group)
    def _(j):
        q, k = q_head(j), k_all()
        for t in range(n_seq // ATTN_TILE):
            limit = (t + 1) * ATTN_TILE
            sl = slice(t * ATTN_TILE, limit)
            s = masked_scores(k, q[sl], limit, ATTN_TILE, scale)
            top = jnp.max(s, axis=0, keepdims=True)
            e = jnp.exp(s - top)
            inv = 1.0 / jnp.sum(e, axis=0, keepdims=True)
            mix_t = dot(vt_ref[:, :limit], (e * inv).astype(BF16)).astype(BF16)
            at_ref[block(j, head_dim), sl] = mix_t
            a_ref[sl, block(j, head_dim)] = mix_t.T
            stat_ref[j, 0:1, sl] = top
            stat_ref[j, 1:2, sl] = inv

    mixed = Exchange(at, lambda d: a_ref.at[block(d, seq)], lambda d: a_all.at[d], relay_a, a_ssem, a_rsem)
    mixed.start()
    a_keep = pltpu.make_async_copy(a_ref.at[block(me, seq)], a_all.at[me], loc_sem.at[2])
    a_keep.start()
    heads_across = send(at_ref.at[block(1 - core, half)], at2_ref.at[:, block(core, n_seq)], t_sem.at[0], t_sem.at[1], at.partner)
    heads_across.start()
    at2_ref[:, block(core, n_seq)] = at_ref[block(core, half), :]
    for d in range(n_dev):
        spots = qkv_ref[d, seq:seq + 1, 0:2 * seq].astype(F32)
        angle = freq_ref[...] * (spots[:, :seq] * 256.0 + spots[:, seq:])
        cost_ref[:, d * seq:(d + 1) * seq] = angle
    cost_all = cost_ref[...]
    cost_ref[...] = jnp.cos(cost_all)
    sint_ref[...] = jnp.sin(cost_all)

    for b in range(2):
        for p in range(2):
            second[b][p].wait_recv()
        second_across[b].start()
    own_across.wait_recv()
    for copy in first_across + second_across:
        copy.wait_recv()
    dy_keep.wait()

    def mix_grad(wo_vm, dyk):
        wo_in = pltpu.make_async_copy(wo_ref.at[block(at.chip, n_rows)], wo_vm, mix_sem.at[2])
        wo_in.start()

        def fetch(i, slot):
            step = jnp.where(i == 0, 0, jnp.where(i == 1, 1, jnp.where(i == 2, 3, 2)))
            chip = at.ring(step)
            return chip, pltpu.make_async_copy(dy_all.at[pl.ds(chip * CORES, CORES), core], dyk.at[slot], mix_sem.at[slot])

        fetch(0, 0)[1].start()
        wo_in.wait()

        @pl.loop(0, at.chips)
        def _(i):
            slot = lax.rem(i, 2)

            @pl.when(i == 1)
            def _():
                for b in range(2):
                    again[b].wait_recv()
                    far_across[b].start()

            @pl.when(i == at.chips - 2)
            def _():
                for b in range(2):
                    far_across[b].wait_recv()

            chip, copy = fetch(i, slot)
            copy.wait()

            @pl.when(i < at.chips - 1)
            def _():
                fetch(i + 1, 1 - slot)[1].start()

            rows = dyk[slot].reshape(CORES * seq, width)
            da_ref[block(chip, CORES * seq), :] = dot_nt(rows, wo_vm[...]).astype(BF16)

    pl.run_scoped(mix_grad, pltpu.VMEM((n_rows, width), BF16), pltpu.VMEM((2, CORES, seq, width), BF16))

    dk_ref[...] = jnp.zeros_like(dk_ref)
    dv_ref[...] = jnp.zeros_like(dv_ref)

    def rotate_back(t, cos, sin):
        u, w = t[:quarter], t[quarter:2 * quarter]
        return jnp.concatenate([u * cos + w * sin, w * cos - u * sin, t[2 * quarter:]], axis=0)

    @pl.loop(0, group)
    def _(j):
        @pl.when(j == 1)
        def _():
            hcols.pass_on()

        @pl.when(j == group - 1)
        def _():
            mixed.pass_on()

        q, k, v = q_head(j), k_all(), v_all()
        for t in range(n_seq // ATTN_TILE):
            limit = (t + 1) * ATTN_TILE
            sl = slice(t * ATTN_TILE, limit)
            da = da_ref[sl, block(j, head_dim)]
            s = masked_scores(k, q[sl], limit, ATTN_TILE, scale)
            p = jnp.exp(s - stat_ref[j, 0:1, sl]) * stat_ref[j, 1:2, sl]
            dp = dot_nt(v[:limit], da)
            row_dot = jnp.sum(p * dp, axis=0, keepdims=True)
            ds = (p * (dp - row_dot) * scale).astype(BF16)
            dv_ref[:limit, :] += dot(p.astype(BF16), da)
            dk_ref[:limit, :] += dot(ds, q[sl])
            back = rotate_back(dot(kt_ref[:, :limit], ds), cost_ref[:, sl], sint_ref[:, sl])
            g_ref[sl, block(j, head_dim)] = back.T.astype(BF16)

    g_ref[:, n_rows:n_rows + head_dim] = rotate_back(dk_ref[...].T, cost_ref[...], sint_ref[...]).T.astype(BF16)
    g_ref[:, n_rows + head_dim:] = dv_ref[...].astype(BF16)
    g_keep = pltpu.make_async_copy(g_ref, g_out, loc_sem.at[0])
    g_keep.start()

    heads_across.wait_recv()

    def wo_tile(dy, out):
        pieces = [dy[d, b] for b in range(n_batch) for d in range(n_dev)]
        out[...] = dot(at2_ref[...], jnp.concatenate(pieces, axis=0))

    pltpu.emit_pipeline(
        wo_tile,
        grid=(width // COL_TILE,),
        in_specs=[pl.BlockSpec((n_dev, n_batch, seq, COL_TILE), lambda i: (0, 0, 0, i))],
        out_specs=[pl.BlockSpec((half, COL_TILE), lambda i: (0, i))],
    )(dy_all, dwo_out)

    hcols.wait_recv()
    mixed.wait_recv()
    for copy in first + second[0] + second[1] + again + [own_across] + first_across + second_across + far_across + [heads_across]:
        copy.wait_send()
    for exchange in (qkv, hcols, mixed):
        exchange.wait_send()
    h_keep.wait()
    a_keep.wait()
    g_keep.wait()


def front(n_dev, x, gain, bias, tables, pos_rows, freq, dy, wq, wk, wv, wo):
    n_batch, seq, width = dy.shape
    n_tok = n_batch * seq
    kv_heads = wk.shape[0]
    group, head_dim = wq.shape[0] // kv_heads, wq.shape[2]
    cols = (group + 2) * head_dim
    n_rows = group * head_dim
    half = n_rows // CORES
    n_seq = n_dev * seq
    quarter = head_dim // 4
    dma = pltpu.SemaphoreType.DMA
    vm = pltpu.VMEM
    return pl.pallas_call(
        functools.partial(front_body, n_dev, group),
        out_shape=(sds((n_dev, n_batch, seq, width), BF16), sds((n_dev, half, n_tok), BF16), sds((n_dev, seq, n_rows), BF16), sds((n_seq, cols), BF16), sds((half, width), F32)),
        in_specs=[VM] * 8 + [ANY] * 5,
        out_specs=(ANY,) * 5,
        scratch_shapes=[
            vm((n_tok, width), BF16), vm((width, n_tok), BF16), vm(dy.shape, BF16), vm((n_dev, seq + PAD, cols), BF16), vm((n_dev, seq + PAD, cols), BF16),
            vm((n_seq, n_rows), BF16), vm((n_rows, n_seq), BF16), vm((half, n_batch * n_seq), BF16), vm((group, 8, n_seq), F32), vm((n_seq, n_rows), BF16), vm((n_seq, cols), BF16),
            vm((head_dim, n_seq), BF16), vm((head_dim, n_seq), BF16), vm((n_seq, head_dim), F32), vm((n_seq, head_dim), F32),
            vm((quarter, n_seq), F32), vm((quarter, n_seq), F32),
            vm((2, seq + PAD, cols), BF16), vm((2, half, n_tok), BF16), vm((2, seq, n_rows), BF16),
            dma((15,)), dma((15,)), dma((9,)), dma((n_dev + 2,)), dma((9,)), dma((n_dev + 2,)), dma((9,)), dma((n_dev + 2,)), dma((2,)), dma((3,)), dma((3,)),
        ],
        compiler_params=pltpu.CompilerParams(collective_id=0, has_side_effects=True, vmem_limit_bytes=VMEM_LIMIT),
        cost_estimate=pl.CostEstimate(flops=10 ** 11, bytes_accessed=10 ** 8, transcendentals=0),
        name='front',
    )(x.reshape(n_tok, width), gain.reshape(1, width), bias.reshape(1, width), *tables, pos_rows, freq.reshape(quarter, 1), dy, wq, wk, wv, wo)


def back_body(n_dev, group, x_ref, dy_ref, gain_ref, g_own, a_all, ht_all, wq_ref, wk_ref, wv_ref, wo_ref,
              out_ref, dx_ref, dwq_out, dwk_out, dwv_out, sum_ref,
              g_ref, mix_ref, lhs_ref, w_ref, acc_ref, dxv_ref, tile_ref, part_ref, all_ref,
              g_ssem, g_rsem, s_ssem, s_rsem, loc_sem, w_sem, t_sem):
    at = Place(n_dev)
    n_tok, width = x_ref.shape
    seq = a_all.shape[1]
    n_batch = n_tok // seq
    n_rows = a_all.shape[2]
    head_dim = wq_ref.shape[2]
    half = ht_all.shape[1]
    n_seq = g_own.shape[0]
    part = n_seq // 2
    core, me = at.core, at.me

    meet(at.peers(True))

    def piece(dev, h):
        return g_ref.at[dev, pl.ds(h * part, part)]

    first = [send(g_own.at[pl.ds(h * part, part)], piece(me, h), g_ssem.at[h], g_rsem.at[h], at.dev(step, core)) for h, step in enumerate((1, -1))]
    second = [send(g_own.at[pl.ds((1 - h) * part, part)], piece(me, 1 - h), g_ssem.at[2 + h], g_rsem.at[2 + h], at.dev(step, core)) for h, step in enumerate((1, -1))]
    origin = [at.dev(-1, core), at.dev(1, core)]
    far_dev = at.dev(2, core)
    again = [send(piece(origin[h], h), piece(origin[h], h), g_ssem.at[4 + h], g_rsem.at[4 + h], at.dev(step, core)) for h, step in enumerate((1, -1))]
    own_across = send(g_own, g_ref.at[me], g_ssem.at[6], g_rsem.at[6], at.partner)
    first_across = [send(piece(origin[h], h), piece(origin[h], h), g_ssem.at[7 + h], g_rsem.at[7 + h], at.partner) for h in range(2)]
    second_across = [send(piece(origin[h], 1 - h), piece(origin[h], 1 - h), g_ssem.at[9 + h], g_rsem.at[9 + h], at.partner) for h in range(2)]
    far_across = [send(piece(far_dev, h), piece(far_dev, h), g_ssem.at[11 + h], g_rsem.at[11 + h], at.partner) for h in range(2)]
    for copy in first + second + [own_across]:
        copy.start()
    g_in = pltpu.make_async_copy(g_own, g_ref.at[me], loc_sem.at[0])
    g_in.start()
    mix_in = [pltpu.make_async_copy(a_all.at[s], mix_ref.at[pl.ds((s % n_batch) * seq, seq), pl.ds((s // n_batch) * n_rows, n_rows)], loc_sem.at[1 + s]) for s in range(n_dev)]
    lhs_in = [pltpu.make_async_copy(ht_all.at[d, :, pl.ds(b * seq, seq)], lhs_ref.at[:, pl.ds((b * n_dev + d) * seq, seq)], loc_sem.at[1 + n_dev + b * n_dev + d]) for d in range(n_dev) for b in range(n_batch)]
    for copy in mix_in + lhs_in:
        copy.start()

    def chip_at(i):
        return at.ring(jnp.where(i == 0, 0, jnp.where(i == 1, 1, jnp.where(i == 2, 3, 2))))

    def weights(i, slot):
        chip = chip_at(i)
        return [
            pltpu.make_async_copy(wq_ref.at[block(chip, group)], w_ref.at[slot, pl.ds(0, group)], w_sem.at[slot, 0]),
            pltpu.make_async_copy(wk_ref.at[chip], w_ref.at[slot, group], w_sem.at[slot, 1]),
            pltpu.make_async_copy(wv_ref.at[chip], w_ref.at[slot, group + 1], w_sem.at[slot, 2]),
        ]

    def tiles(i):
        chip = chip_at(i)
        return [
            pltpu.make_async_copy(tile_ref.at[pl.ds(0, group)], dwq_out.at[block(chip, group)], t_sem.at[0]),
            pltpu.make_async_copy(tile_ref.at[group], dwk_out.at[chip], t_sem.at[1]),
            pltpu.make_async_copy(tile_ref.at[group + 1], dwv_out.at[chip], t_sem.at[2]),
        ]

    for copy in mix_in:
        copy.wait()

    def out_tile(wo, x, out):
        out[...] = (x[...].astype(F32) + dot(mix_ref[...], wo[...])).astype(BF16)

    pltpu.emit_pipeline(
        out_tile,
        grid=(width // COL_TILE,),
        in_specs=[pl.BlockSpec((width, COL_TILE), lambda i: (0, i)), pl.BlockSpec((n_tok, COL_TILE), lambda i: (0, i))],
        out_specs=[pl.BlockSpec((n_tok, COL_TILE), lambda i: (0, i))],
    )(wo_ref, x_ref, out_ref)

    for i in range(2):
        for copy in weights(i, i):
            copy.start()
    for copy in lhs_in:
        copy.wait()
    g_in.wait()
    own_across.wait_recv()

    sums = [send(all_ref.at[me], all_ref.at[me], s_ssem.at[j], s_rsem.at[me], peer) for j, peer in enumerate(at.peers(True))]

    @pl.loop(0, at.chips)
    def _(i):
        slot = lax.rem(i, 2)

        @pl.when(i == 1)
        def _():
            for h in range(2):
                first[h].wait_recv()
                again[h].start()
                first_across[h].start()
            for h in range(2):
                second[h].wait_recv()
                second_across[h].start()
            for copy in first_across + second_across:
                copy.wait_recv()

        @pl.when(i == at.chips - 1)
        def _():
            for h in range(2):
                again[h].wait_recv()
                far_across[h].start()
            for h in range(2):
                far_across[h].wait_recv()

        for copy in weights(i, slot):
            copy.wait()
        chip = chip_at(i)
        mine = jnp.concatenate([g_ref[chip * CORES + b, block(me, seq), :] for b in range(n_batch)], axis=0)
        w = jnp.concatenate([w_ref[slot, j] for j in range(group + 2)], axis=1)
        grow = dot_nt(mine, w)

        @pl.when(i == 0)
        def _():
            acc_ref[...] = grow

        @pl.when(i > 0)
        def _():
            acc_ref[...] += grow

        @pl.when(i < at.chips - 2)
        def _():
            for copy in weights(i + 2, slot):
                copy.start()

        @pl.when(i == at.chips - 1)
        def _():
            part_ref[...] = jnp.zeros_like(part_ref)

            @pl.loop(0, n_tok // ROWS)
            def _(step):
                sl = block(step, ROWS)
                hat, inv = layer_norm(x_ref[sl, :].astype(F32), None)
                dh = acc_ref[sl, :]
                gh = dh * (1.0 + gain_ref[...])
                one = jnp.mean(gh, axis=-1, keepdims=True)
                two = jnp.mean(gh * hat, axis=-1, keepdims=True)
                dxv_ref[sl, :] = (dy_ref[sl, :].astype(F32) + inv * (gh - one - hat * two)).astype(BF16)
                dg = dh * hat
                part_ref[0] += dg[0:8] + dg[8:16]
                part_ref[1] += dh[0:8] + dh[8:16]

            all_ref[me, 0:1, :] = jnp.sum(part_ref[0], axis=0, keepdims=True)
            all_ref[me, 1:2, :] = jnp.sum(part_ref[1], axis=0, keepdims=True)
            pltpu.make_async_copy(dxv_ref, dx_ref, loc_sem.at[0]).start()
            for copy in sums:
                copy.start()

        y = dot(lhs_ref[...], g_ref[pl.ds(chip * CORES, CORES)].reshape(n_batch * n_seq, (group + 2) * head_dim))

        @pl.when(i > 0)
        def _():
            for copy in tiles(i - 1):
                copy.wait()

        for j in range(group + 2):
            tile_ref[j] = y[:, j * head_dim:(j + 1) * head_dim]
        for copy in tiles(i):
            copy.start()

    for j in range(1, n_dev):
        source = lax.rem(me + j, n_dev)
        send(all_ref.at[me], all_ref.at[source], s_ssem.at[0], s_rsem.at[source], at.partner).wait_recv()
    total = all_ref[0]
    for d in range(1, n_dev):
        total = total + all_ref[d]
    sum_ref[...] = total
    for copy in sums + first + second + again + [own_across] + first_across + second_across + far_across:
        copy.wait_send()
    for copy in tiles(at.chips - 1):
        copy.wait()
    pltpu.make_async_copy(dxv_ref, dx_ref, loc_sem.at[0]).wait()


def back(n_dev, x, dy, gain, g_own, a_all, ht_all, wq, wk, wv, wo):
    n_batch, seq, width = dy.shape
    n_tok = n_batch * seq
    kv_heads = wk.shape[0]
    group, head_dim = wq.shape[0] // kv_heads, wq.shape[2]
    cols = (group + 2) * head_dim
    half = ht_all.shape[1]
    n_seq = n_dev * seq
    dma = pltpu.SemaphoreType.DMA
    vm = pltpu.VMEM
    return pl.pallas_call(
        functools.partial(back_body, n_dev, group),
        out_shape=(sds((n_tok, width), BF16), sds((n_tok, width), BF16), sds((kv_heads * group, half, head_dim), F32), sds((kv_heads, half, head_dim), F32), sds((kv_heads, half, head_dim), F32), sds((2, width), F32)),
        in_specs=[VM] * 3 + [ANY] * 7,
        out_specs=(ANY,) * 5 + (VM,),
        scratch_shapes=[
            vm((n_dev, n_seq, cols), BF16), vm((n_tok, width), BF16), vm((half, n_dev * n_tok), BF16), vm((2, group + 2, width, head_dim), BF16), vm((n_tok, width), F32), vm((n_tok, width), BF16),
            vm((group + 2, half, head_dim), F32), vm((2, 8, width), F32), vm((n_dev, 2, width), F32),
            dma((13,)), dma((13,)), dma((n_dev,)), dma((n_dev,)), dma((1 + 3 * n_dev,)), dma((2, 3)), dma((3,)),
        ],
        compiler_params=pltpu.CompilerParams(collective_id=1, has_side_effects=True, vmem_limit_bytes=VMEM_LIMIT),
        cost_estimate=pl.CostEstimate(flops=10 ** 11, bytes_accessed=10 ** 8, transcendentals=0),
        name='back',
    )(x.reshape(n_tok, width), dy.reshape(n_tok, width), gain.reshape(1, width), g_own, a_all, ht_all, wq, wk, wv, wo)


def solution(mesh):
    n_dev = mesh.shape['cp']

    def device_step(x_act, d_out, positions, ln_gain, ln_bias, w_query, w_key, w_value, w_out):
        n_batch, seq, width = x_act.shape
        q_heads, (kv_heads, head_dim) = w_query.shape[1], w_key.shape[1:]
        group = q_heads // kv_heads
        quarter = head_dim // 4
        assert n_batch == CORES and n_dev // CORES == kv_heads == 4 and q_heads * head_dim == width

        freq = jnp.exp(jnp.arange(quarter, dtype=F32) * (-2.0 * math.log(ROPE_BASE) / (head_dim // 2)))
        angles = positions.astype(F32).reshape(n_batch * seq, 1) * freq
        cos, sin = jnp.cos(angles), jnp.sin(angles)
        rest = jnp.zeros((n_batch * seq, head_dim - 2 * quarter), F32)
        none = jnp.zeros_like(sin)
        tables = (jnp.concatenate([cos, cos, rest + 1.0], axis=1), jnp.concatenate([-sin, none, rest], axis=1), jnp.concatenate([none, sin, rest], axis=1))
        cols = (group + 2) * head_dim
        pair = jnp.stack([positions // 256, positions % 256], axis=1).astype(BF16).reshape(n_batch, 1, 2 * seq)
        pos_rows = jnp.pad(pair, ((0, 0), (0, PAD - 1), (0, cols - 2 * seq)))
        by_head = lambda t: jnp.transpose(t, (1, 0, 2))
        wq, wk, wv = by_head(w_query), by_head(w_key), by_head(w_value)

        dy_all, ht_all, a_all, g_own, dwo = front(n_dev, x_act, ln_gain, ln_bias, tables, pos_rows, freq, d_out, wq, wk, wv, w_out)
        out, dx, dwq, dwk, dwv, sums = back(n_dev, x_act, d_out, ln_gain, g_own, a_all, ht_all, wq, wk, wv, w_out)
        return (out.reshape(x_act.shape), dx.reshape(x_act.shape), by_head(dwq), by_head(dwk), by_head(dwv), dwo, sums[0], sums[1])

    return jax.shard_map(device_step, mesh=mesh, in_specs=(P('dp', 'cp', None), P('dp', 'cp', None), P('dp', 'cp'), P(None), P(None), P(None, None, None), P(None, None, None), P(None, None, None), P(None, None)), out_specs=(P('dp', 'cp', None), P('dp', 'cp', None), P(('dp', 'cp'), None, None), P(('dp', 'cp'), None, None), P(('dp', 'cp'), None, None), P(('dp', 'cp'), None), P('dp'), P('dp')), check_vma=False)
```

time: 891 us -> 269 us (0.30)
  waiting for transfers between devices: 500 us -> 0 us
  matrix products: 273 us -> 0 us
  Pallas kernels: 0 us -> 236 us
  other arithmetic: 26.3 us -> 2.84 us
  blocking collectives: 22.9 us -> 0 us
  local copies, waits for them, and re-layouts: 49.2 us -> 28.7 us
  between operations: 14.7 us -> 0.71 us
    reduce_scatter x6 -> x0, waiting for transfers between devices: 468 us -> none  [the longest x4 421 us: reduce_rows(): return lax.psum_scatter(values, 'cp', scatter_dimension=0, tiled=True)]
    dot_general x17 -> x0, matrix products: 240 us -> none  [the longest x1 39.8 us: one_tile(): jnp.einsum('bkgql,bqkgd->blkd', grad_score, q_tile, preferred_element_typ...]
    pallas_call x0 -> x2, Pallas kernels: none -> 236 us  [the longest x1 134 us: front(): pl.pallas_call(functools.partial(front_body, n_dev, group), out_shape=(sd...]
    sub x2 -> x0, matrix products: 33 us -> none  [tile_probs(): shifted = jnp.exp(scores - jnp.max(scores, axis=-1, keepdims=True))]
    all_gather x3 -> x0, waiting for transfers between devices: 31.3 us -> none  [the longest x1 21.5 us: device_step(): key_all = lax.all_gather(k_act, 'cp', axis=1, tiled=True)]
    psum x1 -> x0, blocking collectives: 22.9 us -> none  [device_step(): grad_gain = lax.psum(jnp.sum(grad_h * x_hat, axis=(0, 1)), 'cp')]
    concatenate x10 -> x2, local copies, waits for them, and re-layouts: 12.3 us -> 0.15 us  [the longest x1 0.08 us: device_step(): jnp.concatenate([-sin, none, rest], axis=1)]
    unnamed x81 -> x16, local copies, waits for them, and re-layouts: 18.8 us -> 16.5 us
  transfers between devices with their start and end apart: 9 -> 0, of which waited for: 6 -> 0; matrix products, arithmetic and copies ran while one was open for 29% -> 0% of each run, Pallas kernels for 0% -> 0%
where the time goes in v2:
time: 269 us; the launch traced here: 268 us
  Pallas kernels  236 us (88%)
  local copies, waits for them, and re-layouts  28.7 us (11%)
  other arithmetic  2.84 us (1%)
    pallas_call x1, Pallas kernels, front(): pl.pallas_call(functools.partial(front_body, n_dev, group), out_shape=(sd...  134 us
    pallas_call x1, Pallas kernels, back(): pl.pallas_call(functools.partial(back_body, n_dev, group), out_shape=(sds...  102 us
    unnamed x16, local copies, waits for them, and re-layouts  16.5 us
    transpose x1, local copies, waits for them, and re-layouts, device_step(): by_head = lambda t: jnp.transpose(t, (1, 0, 2))  7.15 us

profile of v2, /device:TPU:81, one launch (start us, length us, event | category | flops | bytes accessed | tf_op | source)
XLA Modules:
  0.0 268.4 jit_solution(2939041370787849516)
XLA Ops:
  0.6 0.1 pad.15.clone
  0.7 0.1 pad.12.clone
  0.8 0.8 fusion.4
  1.6 1.3 reshape.68.gain_ref
  2.9 1.3 reshape.69.bias_ref
  4.3 0.6 multiply_exponential_fusion.freq_ref
  4.9 0.6 pad.4.pos_ref
  5.5 0.5 multiply_sine_fusion
  6.1 0.9 maximum_maximum_fusion.2
  7.0 7.1 %copy_bitcast_fusion = (bf16[4,3584,128]{2,1,0:T(8,128)(2,1)}, bf16[4,3584,128]{2,1,0:T(8,128)(2,1)}) fusion(bf16[3584,4,128]{2,1,0:T(4,128)(2,1)} %param.16, bf16[3584,4,128]{2,1,0:T(4,128)(2,1)} %param.15), kind=kLoop, calls=%fused_computation | loop fusion | bytes 14680064 | tf_op jit(solution)/shard_map/transpose | solution.py:599
  14.1 134.4 %front.1 = (bf16[8,2,128,3584]{3,2,1,0:T(8,128)(2,1)}, bf16[8,448,256]{2,1,0:T(8,128)(2,1)}, bf16[8,128,896]{2,1,0:T(8,128)(2,1)}, bf16[1024,1152]{1,0:T(8,128)(2,1)}, f32[448,3584]{1,0:T(8,128)}) custom-call(bf16[256,3584]{1,0:T(8,128)(2,1)} %bitcast.29, f32[1,3584]{1,0:T(1,128)} %reshape.68.gain_ref, f32[1,3584]{1,0:T(1,128)} %reshape.69.bias_ref, ...), custom_call_target="tpu_custom_call" | custom-call | flops 99999997952 | bytes 100000000 | tf_op jit(solution)/shard_map/front/pallas_call | solution.py:362
  148.5 101.7 %back.1 = (bf16[256,3584]{1,0:T(8,128)(2,1)}, bf16[256,3584]{1,0:T(8,128)(2,1)}, f32[28,448,128]{2,1,0:T(8,128)}, f32[4,448,128]{2,1,0:T(8,128)}, f32[4,448,128]{2,1,0:T(8,128)}, /*index=5*/f32[2,3584]{1,0:T(2,128)}) custom-call(bf16[256,3584]{1,0:T(8,128)(2,1)} %bitcast.30, bf16[256,3584]{1,0:T(8,128)(2,1)} %bitcast.31, f32[1,3584]{1,0:T(1,128)} %reshape.68.gain_ref, ...), custom_call_target="tpu_custom_call" | custom-call | flops 99999997952 | bytes 100000000 | tf_op jit(solution)/shard_map/back/pallas_call | solution.py:564
  250.2 0.0 copy-start.2
  250.2 1.6 slice_reduce_fusion
  251.8 0.0 copy-start.1
  251.8 2.8 %copy.25 = f32[448,4,128]{2,1,0:T(4,128)} copy(f32[448,4,128]{2,0,1:T(8,128)} %bitcast.26) | data formatting | bytes 1835008
  254.7 2.7 %copy.26 = f32[448,4,128]{2,1,0:T(4,128)} copy(f32[448,4,128]{2,0,1:T(8,128)} %bitcast.25) | data formatting | bytes 1835008
  257.3 0.0 copy-done.2
  257.4 0.0 copy-start
  257.4 1.2 copy.33
  258.6 0.0 copy-done.1
  258.6 0.0 slice-start
  258.6 1.2 copy.34
  259.8 1.7 copy-done
  261.5 0.0 slice-start.1
  261.5 3.2 %copy.35 = f32[448,28,128]{2,0,1:T(8,128)} copy(f32[448,28,128]{2,0,1:T(8,128)S(1)} %bitcast.22) | data formatting | bytes 12845056
  264.7 0.0 slice-done
  264.7 1.0 slice-done.1
  265.6 2.7 %copy.36 = f32[448,3584]{1,0:T(8,128)} copy(f32[448,3584]{1,0:T(8,128)S(1)} %bitcast.21) | data formatting | bytes 12845056
  (7 shorter events, 0.0 us)
Async XLA Ops:
  250.2 7.1 %copy-start.2 = (bf16[256,3584]{1,0:T(8,128)(2,1)S(1)}, bf16[256,3584]{1,0:T(8,128)(2,1)}, u32[]{:S(2)}) copy-start(bf16[256,3584]{1,0:T(8,128)(2,1)} %get-tuple-element.21) | copy-start | bytes 5505028
  251.8 6.8 %copy-start.1 = (bf16[256,3584]{1,0:T(8,128)(2,1)S(1)}, bf16[256,3584]{1,0:T(8,128)(2,1)}, u32[]{:S(2)}) copy-start(bf16[256,3584]{1,0:T(8,128)(2,1)} %get-tuple-element.22) | copy-start | bytes 5505028
  257.4 4.1 %copy-start = (f32[28,448,128]{2,1,0:T(8,128)S(1)}, f32[28,448,128]{2,1,0:T(8,128)}, u32[]{:S(2)}) copy-start(f32[28,448,128]{2,1,0:T(8,128)} %get-tuple-element.23) | copy-start | bytes 19267588
  258.6 6.1 %slice-start = ((s8[6422528]{0:T(1024)(128)(4,1)}), s8[4194304]{0:T(1024)(128)(4,1)S(1)}, s32[]{:S(2)}) async-start(s8[6422528]{0:T(1024)(128)(4,1)} %bitcast.20), calls=%async_computation | async-start | bytes 8388608
  261.5 4.1 %slice-start.1 = ((s8[6422528]{0:T(1024)(128)(4,1)}), s8[2228224]{0:T(1024)(128)(4,1)S(1)}, s32[]{:S(2)}) async-start(s8[6422528]{0:T(1024)(128)(4,1)} %bitcast.20), calls=%async_computation.1 | async-start | bytes 4456448

commit v3 on v2

--- a/solution.py
+++ b/solution.py
@@ -2,6 +2,7 @@
 import math
 import jax
 import jax.numpy as jnp
+import numpy as np
 from jax import lax
 from jax.experimental import pallas as pl
 from jax.experimental.pallas import tpu as pltpu
@@ -16,7 +17,6 @@
 ANY = pl.BlockSpec(memory_space=pl.ANY)
 VM = pl.BlockSpec(memory_space=pltpu.VMEM)
 CORES = 2
-PAD = 8
 ATTN_TILE = 256
 COL_TILE = 512
 ROWS = 16
@@ -98,7 +98,7 @@
             copy.wait_send()
 
 
-def layer_norm(x, gain, bias=None):
+def layer_norm(x):
     cen = x - jnp.mean(x, axis=-1, keepdims=True)
     inv = lax.rsqrt(jnp.mean(cen * cen, axis=-1, keepdims=True) + EPS)
     return cen * inv, inv
@@ -112,11 +112,11 @@
     return tail if limit == tile else jnp.concatenate([s[:limit - tile], tail], axis=0)
 
 
-def front_body(n_dev, group, x_ref, gain_ref, bias_ref, cos_ref, sa_ref, sb_ref, pos_ref, freq_ref, dy_ref, wq_ref, wk_ref, wv_ref, wo_ref,
-               dy_all, ht_all, a_all, g_out, dwo_out,
+def front_body(n_dev, group, x_ref, gain_ref, bias_ref, pos_ref, freq_ref, dy_ref, wq_ref, wk_ref, wv_ref, wo_ref,
+               dy_all, ht_all, a_all, g_out, dwo_out, wkv_out,
                h_ref, ht_ref, dyo_ref, qs_ref, qkv_ref, a_ref, at_ref, at2_ref, stat_ref, da_ref, g_ref, kt_ref, vt_ref, dk_ref, dv_ref,
-               cost_ref, sint_ref, relay_q, relay_h, relay_a,
-               dy_ssem, dy_rsem, q_ssem, q_rsem, h_ssem, h_rsem, a_ssem, a_rsem, t_sem, loc_sem, mix_sem):
+               cost_ref, sint_ref, tab_ref, spot_ref, relay_q, relay_h, relay_a,
+               dy_ssem, dy_rsem, q_ssem, q_rsem, h_ssem, h_rsem, a_ssem, a_rsem, p_ssem, p_rsem, t_sem, loc_sem, mix_sem):
     at = Place(n_dev)
     n_batch, seq, width = dy_ref.shape
     n_tok = n_batch * seq
@@ -129,7 +129,7 @@
     scale = head_dim ** -0.5
     core, me = at.core, at.me
 
-    meet(at.peers(False))
+    meet(at.peers(True))
 
     sub = seq // 2
     first = [send(dy_ref.at[b], dy_all.at[me, b], dy_ssem.at[b], dy_rsem.at[b], at.dev(step, core)) for b, step in enumerate((1, -1))]
@@ -145,36 +145,72 @@
         first[b].start()
         second[b][0].start()
     own_across.start()
+    spots = [send(pos_ref, spot_ref.at[me], p_ssem.at[j], p_rsem.at[me], peer) for j, peer in enumerate(at.peers(True))]
+    for copy in spots:
+        copy.start()
     dy_in = pltpu.make_async_copy(dy_ref, dyo_ref, loc_sem.at[0])
     dy_in.start()
+    spot_ref[me] = pos_ref[...]
+
+    freq = freq_ref[...]
+    for b in range(n_batch):
+        angle = freq * pos_ref[b:b + 1, :].astype(F32)
+        cos, sin, none = jnp.cos(angle), jnp.sin(angle), jnp.zeros((quarter, seq), F32)
+        rest = jnp.zeros((head_dim - 2 * quarter, seq), F32)
+        for i, rows in enumerate(([cos, cos, rest + 1.0], [-sin, none, rest], [none, sin, rest])):
+            tab_ref[i, b * seq:(b + 1) * seq, :] = jnp.concatenate(rows, axis=0).T
+
+    gain = (1.0 + gain_ref[...]).reshape(1, width)
+    bias = bias_ref[...].reshape(1, width)
 
     @pl.loop(0, n_tok // ROWS)
     def _(step):
         sl = block(step, ROWS)
-        hat, _ = layer_norm(x_ref[sl, :].astype(F32), None)
-        h_ref[sl, :] = (hat * (1.0 + gain_ref[...]) + bias_ref[...]).astype(BF16)
-
-    def project(wq, wk, wv):
-        chip = pl.program_id(0)
-        slabs = [wq[j] for j in range(group)] + [wk[0], wv[0]]
-        y = dot(h_ref[...], jnp.concatenate(slabs, axis=1))
-        cos, sa, sb = cos_ref[...], sa_ref[...], sb_ref[...]
-        for j in range(group + 2):
-            v = y[:, j * head_dim:(j + 1) * head_dim]
-            if j < group + 1:
-                v = v * cos + pltpu.roll(v, head_dim - quarter, 1) * sa + pltpu.roll(v, quarter, 1) * sb
-            v = v.astype(BF16)
-            for b in range(n_batch):
-                qs_ref[chip * n_batch + b, 0:seq, j * head_dim:(j + 1) * head_dim] = v[b * seq:(b + 1) * seq]
-        for b in range(n_batch):
-            qs_ref[chip * n_batch + b, seq:, :] = pos_ref[b]
-
-    pltpu.emit_pipeline(
-        project,
-        grid=(at.chips,),
-        in_specs=[pl.BlockSpec((group, width, head_dim), lambda i: (i, 0, 0)), pl.BlockSpec((1, width, head_dim), lambda i: (i, 0, 0)), pl.BlockSpec((1, width, head_dim), lambda i: (i, 0, 0))],
-        out_specs=[],
-    )(wq_ref, wk_ref, wv_ref)
+        hat, _ = layer_norm(x_ref[sl, :].astype(F32))
+        h_ref[sl, :] = (hat * gain + bias).astype(BF16)
+
+    def project_all(wkv_ref, raw_ref):
+        raw_in = [pltpu.make_async_copy(w, raw_ref.at[i], mix_sem.at[i]) for i, w in enumerate((wk_ref, wv_ref))]
+        for copy in raw_in:
+            copy.start()
+        for copy in raw_in:
+            copy.wait()
+        span = 64 * at.chips
+        row = lax.broadcasted_iota(jnp.int32, (span, span), 0)
+        col = lax.broadcasted_iota(jnp.int32, (span, span), 1)
+        pick = jnp.where(col == lax.rem(row, 64) * at.chips + lax.div(row, 64), 1.0, 0.0).astype(BF16)
+
+        @pl.loop(0, width // 64)
+        def _(step):
+            sl = block(step, span)
+            rows = dot(pick, jnp.concatenate([raw_ref[0, sl, :], raw_ref[1, sl, :]], axis=1)).astype(BF16)
+            for n in range(at.chips):
+                wkv_ref[n, block(step, 64), :] = rows[n * 64:(n + 1) * 64]
+
+        keep = pltpu.make_async_copy(wkv_ref, wkv_out, mix_sem.at[2])
+        keep.start()
+
+        def project(wq):
+            chip = pl.program_id(0)
+            y = dot(h_ref[...], jnp.concatenate([wq[j] for j in range(group)] + [wkv_ref[chip]], axis=1))
+            cos, sa, sb = tab_ref[0], tab_ref[1], tab_ref[2]
+            for j in range(group + 2):
+                v = y[:, j * head_dim:(j + 1) * head_dim]
+                if j < group + 1:
+                    v = v * cos + pltpu.roll(v, head_dim - quarter, 1) * sa + pltpu.roll(v, quarter, 1) * sb
+                v = v.astype(BF16)
+                for b in range(n_batch):
+                    qs_ref[chip * n_batch + b, :, j * head_dim:(j + 1) * head_dim] = v[b * seq:(b + 1) * seq]
+
+        pltpu.emit_pipeline(
+            project,
+            grid=(at.chips,),
+            in_specs=[pl.BlockSpec((group, width, head_dim), lambda i: (i, 0, 0))],
+            out_specs=[],
+        )(wq_ref)
+        keep.wait()
+
+    pl.run_scoped(project_all, pltpu.VMEM((at.chips, width, 2 * head_dim), BF16), pltpu.VMEM((2, at.chips * width, head_dim), BF16))
 
     qkv = Exchange(at, lambda d: qs_ref.at[d], lambda d: qkv_ref.at[d], relay_q, q_ssem, q_rsem)
     qkv.start()
@@ -201,9 +237,9 @@
     h_keep.start()
 
     qkv.wait_recv()
-    k_all = lambda: qkv_ref[:, 0:seq, n_rows:n_rows + head_dim].reshape(n_seq, head_dim)
-    v_all = lambda: qkv_ref[:, 0:seq, n_rows + head_dim:].reshape(n_seq, head_dim)
-    q_head = lambda j: qkv_ref[:, 0:seq, block(j, head_dim)].reshape(n_seq, head_dim)
+    k_all = lambda: qkv_ref[:, :, n_rows:n_rows + head_dim].reshape(n_seq, head_dim)
+    v_all = lambda: qkv_ref[:, :, n_rows + head_dim:].reshape(n_seq, head_dim)
+    q_head = lambda j: qkv_ref[:, :, block(j, head_dim)].reshape(n_seq, head_dim)
     kt_ref[...] = k_all().T
     vt_ref[...] = v_all().T
 
@@ -230,13 +266,13 @@
     heads_across = send(at_ref.at[block(1 - core, half)], at2_ref.at[:, block(core, n_seq)], t_sem.at[0], t_sem.at[1], at.partner)
     heads_across.start()
     at2_ref[:, block(core, n_seq)] = at_ref[block(core, half), :]
+    for j in range(1, n_dev):
+        source = lax.rem(me + j, n_dev)
+        send(pos_ref, spot_ref.at[source], p_ssem.at[0], p_rsem.at[source], at.partner).wait_recv()
     for d in range(n_dev):
-        spots = qkv_ref[d, seq:seq + 1, 0:2 * seq].astype(F32)
-        angle = freq_ref[...] * (spots[:, :seq] * 256.0 + spots[:, seq:])
-        cost_ref[:, d * seq:(d + 1) * seq] = angle
-    cost_all = cost_ref[...]
-    cost_ref[...] = jnp.cos(cost_all)
-    sint_ref[...] = jnp.sin(cost_all)
+        angle = freq * spot_ref[d, pl.ds(core, 1), :].astype(F32)
+        cost_ref[:, d * seq:(d + 1) * seq] = jnp.cos(angle)
+        sint_ref[:, d * seq:(d + 1) * seq] = jnp.sin(angle)
 
     for b in range(2):
         for p in range(2):
@@ -338,7 +374,7 @@
 
     hcols.wait_recv()
     mixed.wait_recv()
-    for copy in first + second[0] + second[1] + again + [own_across] + first_across + second_across + far_across + [heads_across]:
+    for copy in first + second[0] + second[1] + again + [own_across] + first_across + second_across + far_across + [heads_across] + spots:
         copy.wait_send()
     for exchange in (qkv, hcols, mixed):
         exchange.wait_send()
@@ -347,11 +383,12 @@
     g_keep.wait()
 
 
-def front(n_dev, x, gain, bias, tables, pos_rows, freq, dy, wq, wk, wv, wo):
+def front(n_dev, x, gain, bias, positions, freq, dy, wq, wk, wv, wo):
     n_batch, seq, width = dy.shape
     n_tok = n_batch * seq
-    kv_heads = wk.shape[0]
-    group, head_dim = wq.shape[0] // kv_heads, wq.shape[2]
+    head_dim = wq.shape[2]
+    chips = n_dev // CORES
+    group = wq.shape[0] // chips
     cols = (group + 2) * head_dim
     n_rows = group * head_dim
     half = n_rows // CORES
@@ -361,27 +398,27 @@
     vm = pltpu.VMEM
     return pl.pallas_call(
         functools.partial(front_body, n_dev, group),
-        out_shape=(sds((n_dev, n_batch, seq, width), BF16), sds((n_dev, half, n_tok), BF16), sds((n_dev, seq, n_rows), BF16), sds((n_seq, cols), BF16), sds((half, width), F32)),
-        in_specs=[VM] * 8 + [ANY] * 5,
-        out_specs=(ANY,) * 5,
+        out_shape=(sds((n_dev, n_batch, seq, width), BF16), sds((n_dev, half, n_tok), BF16), sds((n_dev, seq, n_rows), BF16), sds((n_seq, cols), BF16), sds((half, width), F32), sds((chips, width, 2 * head_dim), BF16)),
+        in_specs=[VM] * 5 + [ANY] * 5,
+        out_specs=(ANY,) * 6,
         scratch_shapes=[
-            vm((n_tok, width), BF16), vm((width, n_tok), BF16), vm(dy.shape, BF16), vm((n_dev, seq + PAD, cols), BF16), vm((n_dev, seq + PAD, cols), BF16),
+            vm((n_tok, width), BF16), vm((width, n_tok), BF16), vm(dy.shape, BF16), vm((n_dev, seq, cols), BF16), vm((n_dev, seq, cols), BF16),
             vm((n_seq, n_rows), BF16), vm((n_rows, n_seq), BF16), vm((half, n_batch * n_seq), BF16), vm((group, 8, n_seq), F32), vm((n_seq, n_rows), BF16), vm((n_seq, cols), BF16),
             vm((head_dim, n_seq), BF16), vm((head_dim, n_seq), BF16), vm((n_seq, head_dim), F32), vm((n_seq, head_dim), F32),
-            vm((quarter, n_seq), F32), vm((quarter, n_seq), F32),
-            vm((2, seq + PAD, cols), BF16), vm((2, half, n_tok), BF16), vm((2, seq, n_rows), BF16),
-            dma((15,)), dma((15,)), dma((9,)), dma((n_dev + 2,)), dma((9,)), dma((n_dev + 2,)), dma((9,)), dma((n_dev + 2,)), dma((2,)), dma((3,)), dma((3,)),
+            vm((quarter, n_seq), F32), vm((quarter, n_seq), F32), vm((3, n_tok, head_dim), F32), vm((n_dev, n_batch, seq), jnp.int32),
+            vm((2, seq, cols), BF16), vm((2, half, n_tok), BF16), vm((2, seq, n_rows), BF16),
+            dma((15,)), dma((15,)), dma((9,)), dma((n_dev + 2,)), dma((9,)), dma((n_dev + 2,)), dma((9,)), dma((n_dev + 2,)), dma((n_dev,)), dma((n_dev,)), dma((2,)), dma((3,)), dma((3,)),
         ],
         compiler_params=pltpu.CompilerParams(collective_id=0, has_side_effects=True, vmem_limit_bytes=VMEM_LIMIT),
         cost_estimate=pl.CostEstimate(flops=10 ** 11, bytes_accessed=10 ** 8, transcendentals=0),
         name='front',
-    )(x.reshape(n_tok, width), gain.reshape(1, width), bias.reshape(1, width), *tables, pos_rows, freq.reshape(quarter, 1), dy, wq, wk, wv, wo)
-
-
-def back_body(n_dev, group, x_ref, dy_ref, gain_ref, g_own, a_all, ht_all, wq_ref, wk_ref, wv_ref, wo_ref,
-              out_ref, dx_ref, dwq_out, dwk_out, dwv_out, sum_ref,
-              g_ref, mix_ref, lhs_ref, w_ref, acc_ref, dxv_ref, tile_ref, part_ref, all_ref,
-              g_ssem, g_rsem, s_ssem, s_rsem, loc_sem, w_sem, t_sem):
+    )(x.reshape(n_tok, width), gain, bias, positions, freq, dy, wq, wk, wv, wo)
+
+
+def back_body(n_dev, group, x_ref, dy_ref, gain_ref, g_own, a_all, ht_all, wq_ref, wkv_ref, wo_ref,
+              out_ref, dx_ref, dwq_out, dwk_out, dwv_out, dgain_ref, dbias_ref,
+              g_ref, mix_ref, lhs_ref, w_ref, wkv2_ref, acc_ref, hat_ref, inv_ref, dxv_ref, tile_ref, kv_ref, part_ref, all_ref,
+              g_ssem, g_rsem, r_ssem, r_rsem, x_ssem, x_rsem, s_ssem, s_rsem, loc_sem, w_sem, t_sem):
     at = Place(n_dev)
     n_tok, width = x_ref.shape
     seq = a_all.shape[1]
@@ -390,25 +427,31 @@
     head_dim = wq_ref.shape[2]
     half = ht_all.shape[1]
     n_seq = g_own.shape[0]
-    part = n_seq // 2
+    chips = at.chips
+    part = n_seq // chips
+    cols = (group + 2) * head_dim
     core, me = at.core, at.me
 
     meet(at.peers(True))
 
-    def piece(dev, h):
-        return g_ref.at[dev, pl.ds(h * part, part)]
-
-    first = [send(g_own.at[pl.ds(h * part, part)], piece(me, h), g_ssem.at[h], g_rsem.at[h], at.dev(step, core)) for h, step in enumerate((1, -1))]
-    second = [send(g_own.at[pl.ds((1 - h) * part, part)], piece(me, 1 - h), g_ssem.at[2 + h], g_rsem.at[2 + h], at.dev(step, core)) for h, step in enumerate((1, -1))]
+    def piece(dev, q):
+        return g_ref.at[dev, block(q, part)]
+
+    steps = (1, -1)
+    turn = [[at.ring(2 + q) for q in range(chips)], [at.ring(q) for q in range(chips)]]
+    direct = [[send(g_own.at[block(turn[i][q], part)], piece(me, turn[i][q]), g_ssem.at[i, q], g_rsem.at[i, q], at.dev(steps[i], core)) for q in range(chips)] for i in range(2)]
     origin = [at.dev(-1, core), at.dev(1, core)]
+    came = [[at.ring(1 + q) for q in range(chips)], [at.ring(1 + q) for q in range(chips)]]
+    again = [[send(piece(origin[i], came[i][q]), piece(origin[i], came[i][q]), r_ssem.at[i, q], r_rsem.at[i, q], at.dev(steps[i], core)) for q in range(2)] for i in range(2)]
     far_dev = at.dev(2, core)
-    again = [send(piece(origin[h], h), piece(origin[h], h), g_ssem.at[4 + h], g_rsem.at[4 + h], at.dev(step, core)) for h, step in enumerate((1, -1))]
-    own_across = send(g_own, g_ref.at[me], g_ssem.at[6], g_rsem.at[6], at.partner)
-    first_across = [send(piece(origin[h], h), piece(origin[h], h), g_ssem.at[7 + h], g_rsem.at[7 + h], at.partner) for h in range(2)]
-    second_across = [send(piece(origin[h], 1 - h), piece(origin[h], 1 - h), g_ssem.at[9 + h], g_rsem.at[9 + h], at.partner) for h in range(2)]
-    far_across = [send(piece(far_dev, h), piece(far_dev, h), g_ssem.at[11 + h], g_rsem.at[11 + h], at.partner) for h in range(2)]
-    for copy in first + second + [own_across]:
-        copy.start()
+    ends = [[at.ring(q) for q in range(2)], [at.ring(2 + q) for q in range(2)]]
+    own_across = send(g_own, g_ref.at[me], x_ssem.at[0], x_rsem.at[0], at.partner)
+    near_across = [send(g_ref.at[origin[i]], g_ref.at[origin[i]], x_ssem.at[1 + i], x_rsem.at[1 + i], at.partner) for i in range(2)]
+    far_across = [[send(piece(far_dev, ends[i][q]), piece(far_dev, ends[i][q]), x_ssem.at[3 + 2 * i + q], x_rsem.at[3 + 2 * i + q], at.partner) for q in range(2)] for i in range(2)]
+    for q in range(chips):
+        for i in range(2):
+            direct[i][q].start()
+    own_across.start()
     g_in = pltpu.make_async_copy(g_own, g_ref.at[me], loc_sem.at[0])
     g_in.start()
     mix_in = [pltpu.make_async_copy(a_all.at[s], mix_ref.at[pl.ds((s % n_batch) * seq, seq), pl.ds((s // n_batch) * n_rows, n_rows)], loc_sem.at[1 + s]) for s in range(n_dev)]
@@ -422,18 +465,21 @@
     def weights(i, slot):
         chip = chip_at(i)
         return [
-            pltpu.make_async_copy(wq_ref.at[block(chip, group)], w_ref.at[slot, pl.ds(0, group)], w_sem.at[slot, 0]),
-            pltpu.make_async_copy(wk_ref.at[chip], w_ref.at[slot, group], w_sem.at[slot, 1]),
-            pltpu.make_async_copy(wv_ref.at[chip], w_ref.at[slot, group + 1], w_sem.at[slot, 2]),
+            pltpu.make_async_copy(wq_ref.at[block(chip, group)], w_ref.at[slot], w_sem.at[slot, 0]),
+            pltpu.make_async_copy(wkv_ref.at[chip], wkv2_ref.at[slot], w_sem.at[slot, 1]),
         ]
 
     def tiles(i):
-        chip = chip_at(i)
-        return [
-            pltpu.make_async_copy(tile_ref.at[pl.ds(0, group)], dwq_out.at[block(chip, group)], t_sem.at[0]),
-            pltpu.make_async_copy(tile_ref.at[group], dwk_out.at[chip], t_sem.at[1]),
-            pltpu.make_async_copy(tile_ref.at[group + 1], dwv_out.at[chip], t_sem.at[2]),
-        ]
+        return pltpu.make_async_copy(tile_ref, dwq_out.at[block(chip_at(i), group)], t_sem.at[0])
+
+    gain = (1.0 + gain_ref[...]).reshape(1, width)
+
+    @pl.loop(0, n_tok // ROWS)
+    def _(step):
+        sl = block(step, ROWS)
+        hat, inv = layer_norm(x_ref[sl, :].astype(F32))
+        hat_ref[sl, :] = hat
+        inv_ref[sl, :] = jnp.broadcast_to(inv, (ROWS, 128))
 
     for copy in mix_in:
         copy.wait()
@@ -455,39 +501,39 @@
         copy.wait()
     g_in.wait()
     own_across.wait_recv()
-
     sums = [send(all_ref.at[me], all_ref.at[me], s_ssem.at[j], s_rsem.at[me], peer) for j, peer in enumerate(at.peers(True))]
-
-    @pl.loop(0, at.chips)
+    last = chips - 1
+
+    @pl.loop(0, chips)
     def _(i):
         slot = lax.rem(i, 2)
+        chip = chip_at(i)
 
         @pl.when(i == 1)
         def _():
-            for h in range(2):
-                first[h].wait_recv()
-                again[h].start()
-                first_across[h].start()
-            for h in range(2):
-                second[h].wait_recv()
-                second_across[h].start()
-            for copy in first_across + second_across:
+            for q in range(2):
+                for j in range(2):
+                    direct[j][q].wait_recv()
+                    again[j][q].start()
+            for j in range(2):
+                for q in range(2, chips):
+                    direct[j][q].wait_recv()
+                near_across[j].start()
+            for copy in near_across:
                 copy.wait_recv()
 
-        @pl.when(i == at.chips - 1)
-        def _():
-            for h in range(2):
-                again[h].wait_recv()
-                far_across[h].start()
-            for h in range(2):
-                far_across[h].wait_recv()
+        @pl.when(i == last)
+        def _():
+            for j in range(2):
+                again[j][0].wait_recv()
+                far_across[j][0].start()
+            for j in range(2):
+                far_across[j][0].wait_recv()
 
         for copy in weights(i, slot):
             copy.wait()
-        chip = chip_at(i)
         mine = jnp.concatenate([g_ref[chip * CORES + b, block(me, seq), :] for b in range(n_batch)], axis=0)
-        w = jnp.concatenate([w_ref[slot, j] for j in range(group + 2)], axis=1)
-        grow = dot_nt(mine, w)
+        grow = dot_nt(mine, jnp.concatenate([w_ref[slot, j] for j in range(group)] + [wkv2_ref[slot]], axis=1))
 
         @pl.when(i == 0)
         def _():
@@ -497,25 +543,26 @@
         def _():
             acc_ref[...] += grow
 
-        @pl.when(i < at.chips - 2)
+        @pl.when(i < chips - 2)
         def _():
             for copy in weights(i + 2, slot):
                 copy.start()
 
-        @pl.when(i == at.chips - 1)
+        @pl.when(i == last)
         def _():
             part_ref[...] = jnp.zeros_like(part_ref)
 
             @pl.loop(0, n_tok // ROWS)
             def _(step):
                 sl = block(step, ROWS)
-                hat, inv = layer_norm(x_ref[sl, :].astype(F32), None)
+                hat = hat_ref[sl, :]
+                inv = inv_ref[sl, 0:1]
                 dh = acc_ref[sl, :]
-                gh = dh * (1.0 + gain_ref[...])
+                dg = dh * hat
+                gh = dh * gain
                 one = jnp.mean(gh, axis=-1, keepdims=True)
-                two = jnp.mean(gh * hat, axis=-1, keepdims=True)
+                two = jnp.mean(dg * gain, axis=-1, keepdims=True)
                 dxv_ref[sl, :] = (dy_ref[sl, :].astype(F32) + inv * (gh - one - hat * two)).astype(BF16)
-                dg = dh * hat
                 part_ref[0] += dg[0:8] + dg[8:16]
                 part_ref[1] += dh[0:8] + dh[8:16]
 
@@ -525,37 +572,63 @@
             for copy in sums:
                 copy.start()
 
-        y = dot(lhs_ref[...], g_ref[pl.ds(chip * CORES, CORES)].reshape(n_batch * n_seq, (group + 2) * head_dim))
-
         @pl.when(i > 0)
         def _():
-            for copy in tiles(i - 1):
-                copy.wait()
-
-        for j in range(group + 2):
-            tile_ref[j] = y[:, j * head_dim:(j + 1) * head_dim]
-        for copy in tiles(i):
-            copy.start()
-
+            tiles(i - 1).wait()
+
+        def gather(halves):
+            rows = [at.ring(q) for q in halves]
+            lhs = [lhs_ref[:, pl.ds(pl.multiple_of(b * n_seq + q * part, part), part)] for b in range(n_batch) for q in rows]
+            rhs = [g_ref[chip * CORES + b, block(q, part), :] for b in range(n_batch) for q in rows]
+            return dot(jnp.concatenate(lhs, axis=1), jnp.concatenate(rhs, axis=0))
+
+        def put(y, add):
+            for j in range(group):
+                v = y[:, j * head_dim:(j + 1) * head_dim]
+                tile_ref[j] = tile_ref[j] + v if add else v
+            for j in range(2):
+                v = y[:, (group + j) * head_dim:(group + j + 1) * head_dim]
+                rows = pl.ds(chip, half, stride=chips)
+                kv_ref[j, rows, :] = kv_ref[j, rows, :] + v if add else v
+
+        put(gather((0, 2)), False)
+
+        @pl.when(i == last)
+        def _():
+            for j in range(2):
+                again[j][1].wait_recv()
+                far_across[j][1].start()
+            for j in range(2):
+                far_across[j][1].wait_recv()
+
+        put(gather((1, 3)), True)
+        tiles(i).start()
+
+    kv_put = [pltpu.make_async_copy(kv_ref.at[j], ref, t_sem.at[1 + j]) for j, ref in enumerate((dwk_out, dwv_out))]
+    for copy in kv_put:
+        copy.start()
     for j in range(1, n_dev):
         source = lax.rem(me + j, n_dev)
         send(all_ref.at[me], all_ref.at[source], s_ssem.at[0], s_rsem.at[source], at.partner).wait_recv()
     total = all_ref[0]
     for d in range(1, n_dev):
         total = total + all_ref[d]
-    sum_ref[...] = total
-    for copy in sums + first + second + again + [own_across] + first_across + second_across + far_across:
+    dgain_ref[...] = total[0:1].reshape(width)
+    dbias_ref[...] = total[1:2].reshape(width)
+    for copy in sums + direct[0] + direct[1] + again[0] + again[1] + [own_across] + near_across + far_across[0] + far_across[1]:
         copy.wait_send()
-    for copy in tiles(at.chips - 1):
+    tiles(last).wait()
+    for copy in kv_put:
         copy.wait()
     pltpu.make_async_copy(dxv_ref, dx_ref, loc_sem.at[0]).wait()
 
 
-def back(n_dev, x, dy, gain, g_own, a_all, ht_all, wq, wk, wv, wo):
+def back(n_dev, x, dy, gain, g_own, a_all, ht_all, wq, wkv, wo):
     n_batch, seq, width = dy.shape
     n_tok = n_batch * seq
-    kv_heads = wk.shape[0]
-    group, head_dim = wq.shape[0] // kv_heads, wq.shape[2]
+    chips, _, pair = wkv.shape
+    head_dim = wq.shape[2]
+    group = wq.shape[0] // chips
     cols = (group + 2) * head_dim
     half = ht_all.shape[1]
     n_seq = n_dev * seq
@@ -563,18 +636,18 @@
     vm = pltpu.VMEM
     return pl.pallas_call(
         functools.partial(back_body, n_dev, group),
-        out_shape=(sds((n_tok, width), BF16), sds((n_tok, width), BF16), sds((kv_heads * group, half, head_dim), F32), sds((kv_heads, half, head_dim), F32), sds((kv_heads, half, head_dim), F32), sds((2, width), F32)),
-        in_specs=[VM] * 3 + [ANY] * 7,
-        out_specs=(ANY,) * 5 + (VM,),
+        out_shape=(sds((n_tok, width), BF16), sds((n_tok, width), BF16), sds((chips * group, half, head_dim), F32), sds((chips * half, head_dim), F32), sds((chips * half, head_dim), F32), sds((width,), F32), sds((width,), F32)),
+        in_specs=[VM] * 3 + [ANY] * 6,
+        out_specs=(ANY,) * 5 + (VM, VM),
         scratch_shapes=[
-            vm((n_dev, n_seq, cols), BF16), vm((n_tok, width), BF16), vm((half, n_dev * n_tok), BF16), vm((2, group + 2, width, head_dim), BF16), vm((n_tok, width), F32), vm((n_tok, width), BF16),
-            vm((group + 2, half, head_dim), F32), vm((2, 8, width), F32), vm((n_dev, 2, width), F32),
-            dma((13,)), dma((13,)), dma((n_dev,)), dma((n_dev,)), dma((1 + 3 * n_dev,)), dma((2, 3)), dma((3,)),
+            vm((n_dev, n_seq, cols), BF16), vm((n_tok, width), BF16), vm((half, n_dev * n_tok), BF16), vm((2, group, width, head_dim), BF16), vm((2, width, pair), BF16), vm((n_tok, width), F32), vm((n_tok, width), F32), vm((n_tok, 128), F32), vm((n_tok, width), BF16),
+            vm((group, half, head_dim), F32), vm((2, chips * half, head_dim), F32), vm((2, 8, width), F32), vm((n_dev, 2, width), F32),
+            dma((2, chips)), dma((2, chips)), dma((2, 2)), dma((2, 2)), dma((7,)), dma((7,)), dma((n_dev,)), dma((n_dev,)), dma((1 + 3 * n_dev,)), dma((2, 2)), dma((3,)),
         ],
         compiler_params=pltpu.CompilerParams(collective_id=1, has_side_effects=True, vmem_limit_bytes=VMEM_LIMIT),
         cost_estimate=pl.CostEstimate(flops=10 ** 11, bytes_accessed=10 ** 8, transcendentals=0),
         name='back',
-    )(x.reshape(n_tok, width), dy.reshape(n_tok, width), gain.reshape(1, width), g_own, a_all, ht_all, wq, wk, wv, wo)
+    )(x.reshape(n_tok, width), dy.reshape(n_tok, width), gain, g_own, a_all, ht_all, wq, wkv, wo)
 
 
 def solution(mesh):
@@ -587,20 +660,14 @@
         quarter = head_dim // 4
         assert n_batch == CORES and n_dev // CORES == kv_heads == 4 and q_heads * head_dim == width
 
-        freq = jnp.exp(jnp.arange(quarter, dtype=F32) * (-2.0 * math.log(ROPE_BASE) / (head_dim // 2)))
-        angles = positions.astype(F32).reshape(n_batch * seq, 1) * freq
-        cos, sin = jnp.cos(angles), jnp.sin(angles)
-        rest = jnp.zeros((n_batch * seq, head_dim - 2 * quarter), F32)
-        none = jnp.zeros_like(sin)
-        tables = (jnp.concatenate([cos, cos, rest + 1.0], axis=1), jnp.concatenate([-sin, none, rest], axis=1), jnp.concatenate([none, sin, rest], axis=1))
-        cols = (group + 2) * head_dim
-        pair = jnp.stack([positions // 256, positions % 256], axis=1).astype(BF16).reshape(n_batch, 1, 2 * seq)
-        pos_rows = jnp.pad(pair, ((0, 0), (0, PAD - 1), (0, cols - 2 * seq)))
+        freq = np.exp(np.arange(quarter) * (-2.0 * math.log(ROPE_BASE) / (head_dim // 2))).astype(np.float32).reshape(quarter, 1)
         by_head = lambda t: jnp.transpose(t, (1, 0, 2))
-        wq, wk, wv = by_head(w_query), by_head(w_key), by_head(w_value)
-
-        dy_all, ht_all, a_all, g_own, dwo = front(n_dev, x_act, ln_gain, ln_bias, tables, pos_rows, freq, d_out, wq, wk, wv, w_out)
-        out, dx, dwq, dwk, dwv, sums = back(n_dev, x_act, d_out, ln_gain, g_own, a_all, ht_all, wq, wk, wv, w_out)
-        return (out.reshape(x_act.shape), dx.reshape(x_act.shape), by_head(dwq), by_head(dwk), by_head(dwv), dwo, sums[0], sums[1])
+        by_row = lambda t: t.reshape(width * kv_heads, head_dim)
+        wq = by_head(w_query)
+
+        dy_all, ht_all, a_all, g_own, dwo, wkv = front(n_dev, x_act, ln_gain, ln_bias, positions, jnp.asarray(freq), d_out, wq, by_row(w_key), by_row(w_value), w_out)
+        out, dx, dwq, dwk, dwv, dgain, dbias = back(n_dev, x_act, d_out, ln_gain, g_own, a_all, ht_all, wq, wkv, w_out)
+        kv_rows = lambda t: t.reshape(width // n_dev, kv_heads, head_dim)
+        return (out.reshape(x_act.shape), dx.reshape(x_act.shape), by_head(dwq), kv_rows(dwk), kv_rows(dwv), dwo, dgain, dbias)
 
     return jax.shard_map(device_step, mesh=mesh, in_specs=(P('dp', 'cp', None), P('dp', 'cp', None), P('dp', 'cp'), P(None), P(None), P(None, None, None), P(None, None, None), P(None, None, None), P(None, None)), out_specs=(P('dp', 'cp', None), P('dp', 'cp', None), P(('dp', 'cp'), None, None), P(('dp', 'cp'), None, None), P(('dp', 'cp'), None, None), P(('dp', 'cp'), None), P('dp'), P('dp')), check_vma=False)

time: 269 us -> 249 us (0.926)
  local copies, waits for them, and re-layouts: 28.7 us -> 15.1 us
  Pallas kernels: 236 us -> 233 us
  other arithmetic: 2.84 us -> 0.01 us
    transpose x1 -> x0, local copies, waits for them, and re-layouts: 7.15 us -> none  [device_step(): by_head = lambda t: jnp.transpose(t, (1, 0, 2))]
    pallas_call x1, Pallas kernels: 102 us -> 94.6 us  [back(): pl.pallas_call(functools.partial(back_body, n_dev, group), out_shape=(sds...]
    pallas_call x1, Pallas kernels: 134 us -> 138 us  [front(): pl.pallas_call(functools.partial(front_body, n_dev, group), out_shape=(sd...]
    unnamed x16 -> x22, local copies, waits for them, and re-layouts: 16.5 us -> 15.1 us
where the time goes in v3:
time: 249 us
  Pallas kernels  233 us (94%)
  local copies, waits for them, and re-layouts  15.1 us (6%)
    pallas_call x1, Pallas kernels, front(): pl.pallas_call(functools.partial(front_body, n_dev, group), out_shape=(sd...  138 us
    pallas_call x1, Pallas kernels, back(): pl.pallas_call(functools.partial(back_body, n_dev, group), out_shape=(sds...  94.6 us
    unnamed x22, local copies, waits for them, and re-layouts  15.1 us

profile of v3, /device:TPU:81, one launch (start us, length us, event | category | flops | bytes accessed | tf_op | source)
XLA Modules:
  0.0 248.7 jit_solution(11141882169875242900)
XLA Ops:
  0.6 138.3 %front.1 = (bf16[8,2,128,3584]{3,2,1,0:T(8,128)(2,1)}, bf16[8,448,256]{2,1,0:T(8,128)(2,1)}, bf16[8,128,896]{2,1,0:T(8,128)(2,1)}, bf16[1024,1152]{1,0:T(8,128)(...) custom-call(bf16[256,3584]{1,0:T(8,128)(2,1)} %bitcast.21, f32[3584]{0:T(1024)} %gain_ref.3, f32[3584]{0:T(1024)} %bias_ref.1, ...), custom_call_target="tpu_custom_call" | custom-call | flops 99999997952 | bytes 100000000 | tf_op jit(solution)/shard_map/front/pallas_call | solution.py:399
  139.0 94.6 %back.1 = (bf16[256,3584]{1,0:T(8,128)(2,1)}, bf16[256,3584]{1,0:T(8,128)(2,1)}, f32[28,448,128]{2,1,0:T(8,128)}, f32[1792,128]{1,0:T(8,128)}, f32[1792,128]{1,0:T(8,128)}, /*index=5*/f32[3584]{0:T(1024)}, f32[3584]{0:T(1024)}) custom-call(bf16[256,3584]{1,0:T(8,128)(2,1)} %bitcast.22, bf16[256,3584]{1,0:T(8,128)(2,1)} %bitcast.23, f32[3584]{0:T(1024)} %gain_ref.3, ...), custom_call_target="tpu_custom_call" | custom-call | flops 99999997952 | bytes 100000000 | tf_op jit(solution)/shard_map/back/pallas_call | solution.py:637
  233.6 0.0 copy-start
  233.6 3.0 %copy.26 = bf16[2,128,3584]{2,1,0:T(8,128)(2,1)} copy(bf16[2,128,3584]{2,1,0:T(8,128)(2,1)} %bitcast.14) | data formatting | bytes 3670016
  236.6 0.0 slice-start
  236.6 3.0 %copy.27 = bf16[2,128,3584]{2,1,0:T(8,128)(2,1)} copy(bf16[2,128,3584]{2,1,0:T(8,128)(2,1)} %bitcast.13) | data formatting | bytes 3670016
  239.6 0.0 copy-done
  239.6 0.0 copy-start.2
  239.6 0.0 copy-start.1
  239.6 0.0 slice-start.1
  239.6 3.3 %copy.28 = f32[448,28,128]{2,0,1:T(8,128)} copy(f32[448,28,128]{2,0,1:T(8,128)S(1)} %bitcast.12) | data formatting | bytes 12845056
  242.8 0.0 copy-done.2
  242.8 0.9 copy.29
  243.8 0.0 copy-done.1
  243.8 0.9 copy.30
  244.7 0.0 slice-done
  244.7 0.0 slice-done.1
  244.7 0.0 copy-start.4
  244.7 0.0 copy-start.3
  244.7 2.7 %copy.31 = f32[448,3584]{1,0:T(8,128)} copy(f32[448,3584]{1,0:T(8,128)S(1)} %bitcast.11) | data formatting | bytes 12845056
  247.5 0.0 copy-done.4
  247.5 0.6 copy.32
  248.1 0.0 copy-done.3
  248.1 0.6 copy.33
  (1 shorter events, 0.0 us)
Async XLA Ops:
  233.6 6.0 %copy-start = (f32[28,448,128]{2,1,0:T(8,128)S(1)}, f32[28,448,128]{2,1,0:T(8,128)}, u32[]{:S(2)}) copy-start(f32[28,448,128]{2,1,0:T(8,128)} %get-tuple-element.26) | copy-start | bytes 19267588
  236.6 8.1 %slice-start = ((s8[6422528]{0:T(1024)(128)(4,1)}), s8[4194304]{0:T(1024)(128)(4,1)S(1)}, s32[]{:S(2)}) async-start(s8[6422528]{0:T(1024)(128)(4,1)} %bitcast.10), calls=%async_computation | async-start | bytes 8388608
  239.6 3.3 %copy-start.2 = (f32[1792,128]{1,0:T(8,128)S(1)}, f32[1792,128]{1,0:T(8,128)}, u32[]{:S(2)}) copy-start(f32[1792,128]{1,0:T(8,128)} %get-tuple-element.27) | copy-start | bytes 2752516
  239.6 4.2 %copy-start.1 = (f32[1792,128]{1,0:T(8,128)S(1)}, f32[1792,128]{1,0:T(8,128)}, u32[]{:S(2)}) copy-start(f32[1792,128]{1,0:T(8,128)} %get-tuple-element.28) | copy-start | bytes 2752516
  239.6 5.1 %slice-start.1 = ((s8[6422528]{0:T(1024)(128)(4,1)}), s8[2228224]{0:T(1024)(128)(4,1)S(1)}, s32[]{:S(2)}) async-start(s8[6422528]{0:T(1024)(128)(4,1)} %bitcast.10), calls=%async_computation.1 | async-start | bytes 4456448
  244.7 2.8 %copy-start.4 = (f32[3584]{0:T(1024)S(1)}, f32[3584]{0:T(1024)}, u32[]{:S(2)}) copy-start(f32[3584]{0:T(1024)} %get-tuple-element.46) | copy-start | bytes 43012
  244.7 3.4 %copy-start.3 = (f32[3584]{0:T(1024)S(1)}, f32[3584]{0:T(1024)}, u32[]{:S(2)}) copy-start(f32[3584]{0:T(1024)} %get-tuple-element.47) | copy-start | bytes 43012

commit v4 on v3

v4 whole, which is shorter than its diff:
```python
import functools
import math
import jax
import jax.numpy as jnp
import numpy as np
from jax import lax
from jax.experimental import pallas as pl
from jax.experimental.pallas import tpu as pltpu
from jax.sharding import PartitionSpec as P

EPS = 1e-5
ROPE_BASE = 10000.0
BF16 = jnp.bfloat16
F32 = jnp.float32
VMEM_LIMIT = 46 * 1024 * 1024
NT = (((1,), (1,)), ((), ()))
ANY = pl.BlockSpec(memory_space=pl.ANY)
VM = pl.BlockSpec(memory_space=pltpu.VMEM)
HBM = pl.BlockSpec(memory_space=pltpu.HBM)
CORES = 2
ATTN_TILE = 256
COL_TILE = 512
ROWS = 16
W_SLOTS = 7
W_ROWS = 512


def dot(a, b):
    return jnp.dot(a, b, preferred_element_type=F32)


def dot_nt(a, b):
    return lax.dot_general(a, b, NT, preferred_element_type=F32)


def sds(shape, dtype):
    return jax.ShapeDtypeStruct(shape, dtype)


def block(i, size):
    return pl.ds(pl.multiple_of(i * size, size), size)


class Place:
    def __init__(self, n_dev):
        self.n_dev = n_dev
        self.chips = n_dev // CORES
        self.me = lax.axis_index('cp')
        self.chip = self.me // CORES
        self.core = self.me % CORES
        self.partner = self.chip * CORES + 1 - self.core

    def ring(self, step):
        return lax.rem(self.chip + self.chips + step, self.chips)

    def dev(self, step, core):
        return self.ring(step) * CORES + core

    def peers(self, far):
        near = [self.partner] + [self.dev(s, c) for s in (1, -1) for c in range(CORES)]
        return near + ([self.dev(2, c) for c in range(CORES)] if far else [])


def send(src, dst, ssem, rsem, to):
    return pltpu.make_async_remote_copy(src_ref=src, dst_ref=dst, send_sem=ssem, recv_sem=rsem, device_id={'cp': to}, device_id_type=pl.DeviceIdType.MESH)


def meet(peers):
    barrier = pltpu.get_barrier_semaphore()
    for peer in peers:
        pl.semaphore_signal(barrier, inc=1, device_id={'cp': peer}, device_id_type=pl.DeviceIdType.MESH)
    pl.semaphore_wait(barrier, len(peers))


class Exchange:
    def __init__(self, at, src, dst, relay, ssem, rsem):
        self.at, self.src, self.dst, self.relay, self.ssem, self.rsem = at, src, dst, relay, ssem, rsem
        near = [(0, 1 - at.core)] + [(s, c) for s in (1, -1) for c in range(CORES)]
        n = at.n_dev
        self.near = [send(src(at.dev(s, c)), dst(at.me), ssem.at[i], rsem.at[at.me], at.dev(s, c)) for i, (s, c) in enumerate(near)]
        self.far = [send(src(at.dev(2, i)), relay.at[i], ssem.at[5 + i], rsem.at[n + i], at.dev(step, at.core)) for i, step in enumerate((1, -1))]
        self.on = [send(relay.at[i], dst(at.dev(-step, at.core)), ssem.at[7 + i], rsem.at[at.dev(-step, at.core)], at.dev(step, i)) for i, step in enumerate((1, -1))]

    def start(self):
        for copy in self.far + self.near:
            copy.start()

    def pass_on(self):
        for far, on in zip(self.far, self.on):
            far.wait_recv()
            on.start()

    def wait_recv(self):
        at = self.at
        for j in range(1, at.n_dev):
            origin = lax.rem(at.me + j, at.n_dev)
            send(self.src(at.me), self.dst(origin), self.ssem.at[0], self.rsem.at[origin], at.partner).wait_recv()

    def wait_send(self):
        for copy in self.far + self.near + self.on:
            copy.wait_send()


def layer_norm(x):
    cen = x - jnp.mean(x, axis=-1, keepdims=True)
    inv = lax.rsqrt(jnp.mean(cen * cen, axis=-1, keepdims=True) + EPS)
    return cen * inv, inv


def masked_scores(k, q, limit, tile, scale):
    s = dot_nt(k[:limit], q) * scale
    row = lax.broadcasted_iota(jnp.int32, (tile, tile), 0)
    col = lax.broadcasted_iota(jnp.int32, (tile, tile), 1)
    tail = jnp.where(row <= col, s[limit - tile:], -1e30)
    return tail if limit == tile else jnp.concatenate([s[:limit - tile], tail], axis=0)


def block_body(n_dev, group, gain_ref, bias_ref, pos_ref, freq_ref, x_hbm, dy_ref, wq_ref, wk_ref, wv_ref, wo_ref,
               out_ref, dx_ref, dwq_ref, dwk_ref, dwv_ref, dwo_ref, dgain_ref, dbias_ref, dy_all, ht_all, a_all, g_all, wkv_all,
               h_ref, ht_ref, qs_ref, qkv_ref, a_ref, at_ref, at2_ref, stat_ref, da_ref, kt_ref, vt_ref, dk_ref, dv_ref,
               cost_ref, sint_ref, tab_ref, spot_ref, relay_q, relay_h, relay_a, far_ref, part_ref, all_ref,
               dy_ssem, dy_rsem, q_ssem, q_rsem, h_ssem, h_rsem, a_ssem, a_rsem, p_ssem, p_rsem, t_sem,
               g_ssem, g_rsem, r_ssem, r_rsem, x_ssem, x_rsem, s_ssem, s_rsem, loc_sem, mix_sem, lhs_sem, w_sem, job_sem):
    at = Place(n_dev)
    n_batch, seq, width = dy_ref.shape
    n_tok = n_batch * seq
    head_dim = wq_ref.shape[2]
    cols = (group + 2) * head_dim
    n_rows = group * head_dim
    half = n_rows // CORES
    n_seq = n_dev * seq
    quarter = head_dim // 4
    scale = head_dim ** -0.5
    chips = at.chips
    core, me = at.core, at.me
    steps = (1, -1)
    origin = [at.dev(-1, core), at.dev(1, core)]
    far_dev = at.dev(2, core)

    meet(at.peers(True))

    sub = seq // 2
    first = [send(dy_ref.at[b], dy_all.at[me, b], dy_ssem.at[b], dy_rsem.at[b], at.dev(steps[b], core)) for b in range(2)]
    second = [[send(dy_ref.at[1 - b, pl.ds(p * sub, sub)], dy_all.at[me, 1 - b, pl.ds(p * sub, sub)], dy_ssem.at[2 + 2 * b + p], dy_rsem.at[2 + 2 * b + p], at.dev(steps[b], core)) for p in range(2)] for b in range(2)]
    again = [send(dy_all.at[origin[b], b], dy_all.at[origin[b], b], dy_ssem.at[6 + b], dy_rsem.at[6 + b], at.dev(steps[b], core)) for b in range(2)]
    own_across = send(dy_ref, dy_all.at[me], dy_ssem.at[8], dy_rsem.at[8], at.partner)
    first_across = [send(dy_all.at[origin[b], b], dy_all.at[origin[b], b], dy_ssem.at[9 + b], dy_rsem.at[9 + b], at.partner) for b in range(2)]
    second_across = [send(dy_all.at[origin[b], 1 - b], dy_all.at[origin[b], 1 - b], dy_ssem.at[11 + b], dy_rsem.at[11 + b], at.partner) for b in range(2)]
    far_across = [send(dy_all.at[far_dev, b], dy_all.at[far_dev, b], dy_ssem.at[13 + b], dy_rsem.at[13 + b], at.partner) for b in range(2)]
    for b in range(2):
        first[b].start()
        second[b][0].start()
    x_in = pltpu.make_async_copy(x_hbm, dx_ref, loc_sem.at[1])
    x_in.start()
    own_across.start()
    spots = [send(pos_ref, spot_ref.at[me], p_ssem.at[j], p_rsem.at[me], peer) for j, peer in enumerate(at.peers(True))]
    for copy in spots:
        copy.start()
    spot_ref[me] = pos_ref[...]

    freq = freq_ref[...]
    for b in range(n_batch):
        angle = freq * pos_ref[b:b + 1, :].astype(F32)
        cos, sin, none = jnp.cos(angle), jnp.sin(angle), jnp.zeros((quarter, seq), F32)
        rest = jnp.zeros((head_dim - 2 * quarter, seq), F32)
        for i, rows in enumerate(([cos, cos, rest + 1.0], [-sin, none, rest], [none, sin, rest])):
            tab_ref[i, b * seq:(b + 1) * seq, :] = jnp.concatenate(rows, axis=0).T

    gain = (1.0 + gain_ref[...]).reshape(1, width)
    bias = bias_ref[...].reshape(1, width)
    x_in.wait()

    @pl.loop(0, n_tok // ROWS)
    def _(step):
        sl = block(step, ROWS)
        hat, _ = layer_norm(dx_ref[sl, :].astype(F32))
        h_ref[sl, :] = (hat * gain + bias).astype(BF16)

    def project_all(wkv_ref, dyo_ref):
        dy_in = pltpu.make_async_copy(dy_ref, dyo_ref, loc_sem.at[0])
        dy_in.start()
        span = 64 * chips
        row = lax.broadcasted_iota(jnp.int32, (span, span), 0)
        col = lax.broadcasted_iota(jnp.int32, (span, span), 1)
        pick = jnp.where(col == lax.rem(row, 64) * chips + lax.div(row, 64), 1.0, 0.0).astype(BF16)
        batch = 4

        def part_heads(wk, wv):
            for i in range(batch):
                sl = slice(i * span, (i + 1) * span)
                rows = dot(pick, jnp.concatenate([wk[sl, :], wv[sl, :]], axis=1)).astype(BF16)
                for n in range(chips):
                    wkv_ref[n, block(pl.program_id(0) * batch + i, 64), :] = rows[n * 64:(n + 1) * 64]

        pltpu.emit_pipeline(part_heads, grid=(width // (64 * batch),), in_specs=[pl.BlockSpec((span * batch, head_dim), lambda i: (i, 0))] * 2, out_specs=[])(wk_ref, wv_ref)
        keep = pltpu.make_async_copy(wkv_ref, wkv_all, mix_sem.at[2])
        keep.start()
        dy_in.wait()
        dy_keep = pltpu.make_async_copy(dyo_ref, dy_all.at[me], loc_sem.at[0])
        dy_keep.start()

        def place(v, chip, j, turn):
            if turn:
                v = v * tab_ref[0] + pltpu.roll(v, head_dim - quarter, 1) * tab_ref[1] + pltpu.roll(v, quarter, 1) * tab_ref[2]
            v = v.astype(BF16)
            for b in range(n_batch):
                qs_ref[chip * n_batch + b, :, block(j, head_dim)] = v[b * seq:(b + 1) * seq]

        def project(wq):
            y = dot(h_ref[...], jnp.concatenate([wq[0], wq[1]], axis=1))
            for i in range(2):
                head = pl.program_id(0) * 2 + i
                place(y[:, i * head_dim:(i + 1) * head_dim], lax.div(head, group), lax.rem(head, group), True)

        pltpu.emit_pipeline(project, grid=(chips * group // 2,), in_specs=[pl.BlockSpec((2, width, head_dim), lambda i: (i, 0, 0))], out_specs=[])(wq_ref)

        @pl.loop(0, chips)
        def _(chip):
            y = dot(h_ref[...], wkv_ref[chip])
            place(y[:, :head_dim], chip, group, True)
            place(y[:, head_dim:], chip, group + 1, False)

        keep.wait()
        dy_keep.wait()

    pl.run_scoped(project_all, pltpu.VMEM((chips, width, 2 * head_dim), BF16), pltpu.VMEM(dy_ref.shape, BF16))

    qkv = Exchange(at, lambda d: qs_ref.at[d], lambda d: qkv_ref.at[d], relay_q, q_ssem, q_rsem)
    qkv.start()
    qkv_ref[me] = qs_ref[me]

    @pl.loop(0, width // 128)
    def _(step):
        sl = block(step, 128)
        ht_ref[sl, :] = h_ref[:, sl].T

    qkv.pass_on()
    for b in range(2):
        second[b][1].start()
    for b in range(2):
        first[b].wait_recv()
        again[b].start()
        first_across[b].start()
    hcols = Exchange(at, lambda d: ht_ref.at[block(d, half)], lambda d: ht_all.at[d], relay_h, h_ssem, h_rsem)
    hcols.start()
    h_keep = pltpu.make_async_copy(ht_ref.at[block(me, half)], ht_all.at[me], loc_sem.at[1])
    h_keep.start()

    qkv.wait_recv()
    k_all = lambda: qkv_ref[:, :, n_rows:n_rows + head_dim].reshape(n_seq, head_dim)
    v_all = lambda: qkv_ref[:, :, n_rows + head_dim:].reshape(n_seq, head_dim)
    q_head = lambda j: qkv_ref[:, :, block(j, head_dim)].reshape(n_seq, head_dim)
    kt_ref[...] = k_all().T
    vt_ref[...] = v_all().T

    @pl.loop(0, group)
    def _(j):
        q, k = q_head(j), k_all()
        for t in range(n_seq // ATTN_TILE):
            limit = (t + 1) * ATTN_TILE
            sl = slice(t * ATTN_TILE, limit)
            s = masked_scores(k, q[sl], limit, ATTN_TILE, scale)
            top = jnp.max(s, axis=0, keepdims=True)
            e = jnp.exp(s - top)
            inv = 1.0 / jnp.sum(e, axis=0, keepdims=True)
            mix_t = dot(vt_ref[:, :limit], (e * inv).astype(BF16)).astype(BF16)
            at_ref[block(j, head_dim), sl] = mix_t
            a_ref[sl, block(j, head_dim)] = mix_t.T
            stat_ref[j, 0:1, sl] = top
            stat_ref[j, 1:2, sl] = inv

    mixed = Exchange(at, lambda d: a_ref.at[block(d, seq)], lambda d: a_all.at[d], relay_a, a_ssem, a_rsem)
    mixed.start()
    a_keep = pltpu.make_async_copy(a_ref.at[block(me, seq)], a_all.at[me], loc_sem.at[2])
    a_keep.start()
    heads_across = send(at_ref.at[block(1 - core, half)], at2_ref.at[:, block(core, n_seq)], t_sem.at[0], t_sem.at[1], at.partner)
    heads_across.start()
    at2_ref[:, block(core, n_seq)] = at_ref[block(core, half), :]
    for j in range(1, n_dev):
        source = lax.rem(me + j, n_dev)
        send(pos_ref, spot_ref.at[source], p_ssem.at[0], p_rsem.at[source], at.partner).wait_recv()
    for d in range(n_dev):
        angle = freq * spot_ref[d, pl.ds(core, 1), :].astype(F32)
        cost_ref[:, d * seq:(d + 1) * seq] = jnp.cos(angle)
        sint_ref[:, d * seq:(d + 1) * seq] = jnp.sin(angle)

    for b in range(2):
        for p in range(2):
            second[b][p].wait_recv()
        second_across[b].start()
    own_across.wait_recv()
    for copy in first_across + second_across:
        copy.wait_recv()

    def chip_at(i):
        return at.ring(jnp.where(i == 0, 0, jnp.where(i == 1, 1, jnp.where(i == 2, 3, 2))))

    def mix_grad(wo_vm, dyk):
        wo_in = pltpu.make_async_copy(wo_ref.at[block(at.chip, n_rows)], wo_vm, mix_sem.at[2])
        wo_in.start()

        def fetch(i, slot):
            return pltpu.make_async_copy(dy_all.at[block(chip_at(i), CORES), core], dyk.at[slot], mix_sem.at[slot])

        fetch(0, 0).start()
        wo_in.wait()

        @pl.loop(0, chips)
        def _(i):
            slot = lax.rem(i, 2)

            @pl.when(i == 1)
            def _():
                for b in range(2):
                    again[b].wait_recv()
                    far_across[b].start()

            @pl.when(i == chips - 2)
            def _():
                for b in range(2):
                    far_across[b].wait_recv()

            fetch(i, slot).wait()

            @pl.when(i < chips - 1)
            def _():
                fetch(i + 1, 1 - slot).start()

            rows = dyk[slot].reshape(CORES * seq, width)
            da_ref[block(chip_at(i), CORES * seq), :] = dot_nt(rows, wo_vm[...]).astype(BF16)

    pl.run_scoped(mix_grad, pltpu.VMEM((n_rows, width), BF16), pltpu.VMEM((2, CORES, seq, width), BF16))

    qkv.wait_send()
    g_ref = qs_ref
    dk_ref[...] = jnp.zeros_like(dk_ref)
    dv_ref[...] = jnp.zeros_like(dv_ref)

    def rotate_back(t, cos, sin):
        u, w = t[:quarter], t[quarter:2 * quarter]
        return jnp.concatenate([u * cos + w * sin, w * cos - u * sin, t[2 * quarter:]], axis=0)

    def by_dev(t):
        return t.astype(BF16).reshape(t.shape[0] // seq, seq, head_dim)

    @pl.loop(0, group)
    def _(j):
        @pl.when(j == 1)
        def _():
            hcols.pass_on()

        @pl.when(j == group - 1)
        def _():
            mixed.pass_on()

        q, k, v = q_head(j), k_all(), v_all()
        for t in range(n_seq // ATTN_TILE):
            limit = (t + 1) * ATTN_TILE
            sl = slice(t * ATTN_TILE, limit)
            da = da_ref[sl, block(j, head_dim)]
            s = masked_scores(k, q[sl], limit, ATTN_TILE, scale)
            p = jnp.exp(s - stat_ref[j, 0:1, sl]) * stat_ref[j, 1:2, sl]
            dp = dot_nt(v[:limit], da)
            row_dot = jnp.sum(p * dp, axis=0, keepdims=True)
            ds = (p * (dp - row_dot) * scale).astype(BF16)
            dv_ref[:limit, :] += dot(p.astype(BF16), da)
            dk_ref[:limit, :] += dot(ds, q[sl])
            back = rotate_back(dot(kt_ref[:, :limit], ds), cost_ref[:, sl], sint_ref[:, sl])
            g_ref[t * ATTN_TILE // seq:limit // seq, :, block(j, head_dim)] = by_dev(back.T)

    g_ref[:, :, n_rows:n_rows + head_dim] = by_dev(rotate_back(dk_ref[...].T, cost_ref[...], sint_ref[...]).T)
    g_ref[:, :, n_rows + head_dim:] = by_dev(dv_ref[...])

    def span_of(q):
        return block(q, CORES)

    turn = [[at.ring(2 + q) for q in range(chips)], [at.ring(q) for q in range(chips)]]
    direct = [[send(g_ref.at[span_of(turn[i][q])], g_all.at[me, span_of(turn[i][q])], g_ssem.at[i, q], g_rsem.at[i, q], at.dev(steps[i], core)) for q in range(chips)] for i in range(2)]
    came = [at.ring(1 + q) for q in range(chips)]
    onward = [[send(g_all.at[origin[i], span_of(came[q])], far_ref.at[core, span_of(came[q])], r_ssem.at[i, q], r_rsem.at[i, q], at.dev(steps[i], core)) for q in range(2)] for i in range(2)]
    ends = [[at.ring(q) for q in range(2)], [at.ring(2 + q) for q in range(2)]]
    g_across = send(g_ref, g_all.at[me], x_ssem.at[0], x_rsem.at[0], at.partner)
    near_across = [[send(g_all.at[origin[i], span_of(came[q])], g_all.at[origin[i], span_of(came[q])], x_ssem.at[1 + i * chips + q], x_rsem.at[1 + i * chips + q], at.partner) for q in range(chips)] for i in range(2)]
    end_across = [[send(far_ref.at[core, span_of(ends[i][q])], far_ref.at[core, span_of(ends[i][q])], x_ssem.at[1 + (2 + i) * chips + q], x_rsem.at[1 + (2 + i) * chips + q], at.partner) for q in range(2)] for i in range(2)]
    for q in range(chips):
        for i in range(2):
            direct[i][q].start()
    g_across.start()
    g_keep = pltpu.make_async_copy(g_ref, g_all.at[me], loc_sem.at[0])
    g_keep.start()

    heads_across.wait_recv()

    def wo_tile(dy):
        pieces = [dy[d, b] for b in range(n_batch) for d in range(n_dev)]
        dwo_ref[:, block(pl.program_id(0), COL_TILE)] = dot(at2_ref[...], jnp.concatenate(pieces, axis=0))

    pltpu.emit_pipeline(wo_tile, grid=(width // COL_TILE,), in_specs=[pl.BlockSpec((n_dev, n_batch, seq, COL_TILE), lambda i: (0, 0, 0, i))], out_specs=[])(dy_all)

    hcols.wait_recv()
    h_keep.wait()
    lhs_in = [pltpu.make_async_copy(ht_all.at[d, :, pl.ds(b * seq, seq)], at2_ref.at[:, pl.ds((b * n_dev + d) * seq, seq)], lhs_sem.at[b * n_dev + d]) for d in range(n_dev) for b in range(n_batch)]
    for copy in lhs_in:
        copy.start()
    mixed.wait_recv()
    a_keep.wait()
    mix_in = [pltpu.make_async_copy(a_all.at[s], h_ref.at[pl.ds((s % n_batch) * seq, seq), pl.ds((s // n_batch) * n_rows, n_rows)], loc_sem.at[1 + s]) for s in range(n_dev)]
    for copy in mix_in:
        copy.start()
    for copy in mix_in:
        copy.wait()

    def out_tile(wo):
        sl = block(pl.program_id(0), COL_TILE)
        out_ref[:, sl] = (dx_ref[:, sl].astype(F32) + dot(h_ref[...], wo[...])).astype(BF16)

    pltpu.emit_pipeline(out_tile, grid=(width // COL_TILE,), in_specs=[pl.BlockSpec((width, COL_TILE), lambda i: (0, i))], out_specs=[])(wo_ref)

    dy_back = [pltpu.make_async_copy(dy_ref.at[b], h_ref.at[pl.ds(b * seq, seq)], loc_sem.at[1 + b]) for b in range(n_batch)]
    for copy in dy_back:
        copy.start()
    for copy in lhs_in:
        copy.wait()
    g_keep.wait()
    g_across.wait_recv()
    sums = [send(all_ref.at[me], all_ref.at[me], s_ssem.at[j], s_rsem.at[me], peer) for j, peer in enumerate(at.peers(True))]

    def weight_grads(wq_vm, wkv_vm, acc_ref, job_ref, mine_ref):
        n_slots = wq_vm.shape[0]
        chunk = wq_vm.shape[2]
        n_chunks = width // chunk
        total = n_chunks * chips

        def weights(s):
            slot = lax.rem(s, n_slots)
            chip = chip_at(lax.div(s, n_chunks))
            rows = block(lax.rem(s, n_chunks), chunk)
            return [
                pltpu.make_async_copy(wq_ref.at[block(chip, group), rows], wq_vm.at[slot], w_sem.at[slot, 0]),
                pltpu.make_async_copy(wkv_all.at[chip, rows], wkv_vm.at[slot], w_sem.at[slot, 1]),
            ]

        for s in range(n_slots):
            for copy in weights(s):
                copy.start()

        def grow(i, read):
            @pl.loop(0, n_chunks)
            def _(n):
                s = i * n_chunks + n
                slot = lax.rem(s, n_slots)
                for copy in weights(s):
                    copy.wait()
                rows = jnp.concatenate([read(b) for b in range(n_batch)], axis=0)
                part = dot_nt(rows, jnp.concatenate([wq_vm[slot, j] for j in range(group)] + [wkv_vm[slot]], axis=1))
                sl = block(n, chunk)

                @pl.when(i == 0)
                def _():
                    acc_ref[:, sl] = part

                @pl.when(i > 0)
                def _():
                    acc_ref[:, sl] += part

                @pl.when(s + n_slots < total)
                def _():
                    for copy in weights(s + n_slots):
                        copy.start()

        def mine_in(chip):
            return [pltpu.make_async_copy(g_all.at[chip * CORES + b, me], mine_ref.at[b], job_sem.at[2, b, 0]) for b in range(n_batch)]

        def grow_near(i):
            copies = mine_in(chip_at(i))
            for copy in copies:
                copy.start()
            for copy in copies:
                copy.wait()
            grow(i, lambda b: mine_ref[b])

        def job_in(chip, quarters, slot):
            return [pltpu.make_async_copy(g_all.at[chip * CORES + b, span_of(q)], job_ref.at[slot, b, n], job_sem.at[slot, b, n]) for b in range(n_batch) for n, q in enumerate(quarters)]

        def job(chip, quarters, read, add):
            part = CORES * seq
            lhs = [at2_ref[:, pl.ds(pl.multiple_of(b * n_seq + q * part, part), part)] for b in range(n_batch) for q in quarters]
            rhs = [read(b, n, q).reshape(part, cols) for b in range(n_batch) for n, q in enumerate(quarters)]
            y = dot(jnp.concatenate(lhs, axis=1), jnp.concatenate(rhs, axis=0))
            for j in range(group):
                v = y[:, j * head_dim:(j + 1) * head_dim]
                dwq_ref[chip * group + j] = dwq_ref[chip * group + j] + v if add else v
            for j, ref in enumerate((dwk_ref, dwv_ref)):
                v = y[:, (group + j) * head_dim:(group + j + 1) * head_dim]
                rows = pl.ds(chip, half, stride=chips)
                ref[rows, :] = ref[rows, :] + v if add else v

        def near_pair(quarters, add):
            for slot, step in enumerate(steps):
                for copy in job_in(at.ring(step), quarters, slot):
                    copy.start()

            @pl.loop(0, 2)
            def _(slot):
                chip = at.ring(1 - 2 * slot)
                for copy in job_in(chip, quarters, slot):
                    copy.wait()
                job(chip, quarters, lambda b, n, q: job_ref[slot, b, n], add)

        for slot in range(2):
            for copy in job_in(at.chip, [at.ring(2 * slot), at.ring(2 * slot + 1)], slot):
                copy.start()
        grow_near(0)
        for slot in range(2):
            quarters = [at.ring(2 * slot), at.ring(2 * slot + 1)]
            for copy in job_in(at.chip, quarters, slot):
                copy.wait()
            job(at.chip, quarters, lambda b, n, q: job_ref[slot, b, n], slot == 1)

        for q in range(2):
            for i in range(2):
                direct[i][q].wait_recv()
                onward[i][q].start()
                near_across[i][q].start()
        for q in range(2):
            for i in range(2):
                near_across[i][q].wait_recv()
        near_pair(came[:2], False)
        for q in range(2, chips):
            for i in range(2):
                direct[i][q].wait_recv()
                near_across[i][q].start()
        for q in range(2, chips):
            for i in range(2):
                near_across[i][q].wait_recv()

        @pl.loop(1, chips - 1)
        def _(i):
            grow_near(i)

        near_pair(came[2:], True)
        far_chip = at.ring(2)
        for i in range(2):
            onward[i][0].wait_recv()
            end_across[i][0].start()
        for i in range(2):
            end_across[i][0].wait_recv()
        grow(chips - 1, lambda b: far_ref[b, me])
        for copy in dy_back:
            copy.wait()
        part_ref[...] = jnp.zeros_like(part_ref)

        @pl.loop(0, n_tok // ROWS)
        def _(step):
            sl = block(step, ROWS)
            hat, inv = layer_norm(dx_ref[sl, :].astype(F32))
            dh = acc_ref[sl, :]
            dg = dh * hat
            gh = dh * gain
            one = jnp.mean(gh, axis=-1, keepdims=True)
            two = jnp.mean(dg * gain, axis=-1, keepdims=True)
            dx_ref[sl, :] = (h_ref[sl, :].astype(F32) + inv * (gh - one - hat * two)).astype(BF16)
            part_ref[0] += dg[0:8] + dg[8:16]
            part_ref[1] += dh[0:8] + dh[8:16]

        all_ref[me, 0:1, :] = jnp.sum(part_ref[0], axis=0, keepdims=True)
        all_ref[me, 1:2, :] = jnp.sum(part_ref[1], axis=0, keepdims=True)
        read_far = lambda b, n, q: far_ref[b, span_of(q)]
        for copy in sums:
            copy.start()
        job(far_chip, [ends[0][0], ends[1][0]], read_far, False)
        for i in range(2):
            onward[i][1].wait_recv()
            end_across[i][1].start()
        for i in range(2):
            end_across[i][1].wait_recv()
        job(far_chip, [ends[0][1], ends[1][1]], read_far, True)

    pl.run_scoped(
        weight_grads,
        pltpu.VMEM((W_SLOTS, group, W_ROWS, head_dim), BF16), pltpu.VMEM((W_SLOTS, W_ROWS, 2 * head_dim), BF16), pltpu.VMEM((n_tok, width), F32),
        pltpu.VMEM((2, n_batch, 2, CORES, seq, cols), BF16), pltpu.VMEM((n_batch, seq, cols), BF16),
    )

    for j in range(1, n_dev):
        source = lax.rem(me + j, n_dev)
        send(all_ref.at[me], all_ref.at[source], s_ssem.at[0], s_rsem.at[source], at.partner).wait_recv()
    total = all_ref[0]
    for d in range(1, n_dev):
        total = total + all_ref[d]
    dgain_ref[...] = total[0:1].reshape(width)
    dbias_ref[...] = total[1:2].reshape(width)
    done = first + second[0] + second[1] + again + [own_across] + first_across + second_across + far_across + [heads_across] + spots
    done += direct[0] + direct[1] + onward[0] + onward[1] + [g_across] + near_across[0] + near_across[1] + end_across[0] + end_across[1] + sums
    for copy in done:
        copy.wait_send()
    hcols.wait_send()
    mixed.wait_send()


def whole_block(n_dev, x, gain, bias, positions, freq, dy, wq, wk, wv, wo):
    n_batch, seq, width = dy.shape
    n_tok = n_batch * seq
    head_dim = wq.shape[2]
    chips = n_dev // CORES
    group = wq.shape[0] // chips
    cols = (group + 2) * head_dim
    n_rows = group * head_dim
    half = n_rows // CORES
    n_seq = n_dev * seq
    quarter = head_dim // 4
    dma = pltpu.SemaphoreType.DMA
    vm = pltpu.VMEM
    shapes = [((n_tok, width), BF16)] * 2 + [((chips * group, half, head_dim), F32)] + [((chips * half, head_dim), F32)] * 2 + [((half, width), F32), ((width,), F32), ((width,), F32)]
    held = [((n_dev, n_batch, seq, width), BF16), ((n_dev, half, n_tok), BF16), ((n_dev, seq, n_rows), BF16), ((n_dev, n_dev, seq, cols), BF16), ((chips, width, 2 * head_dim), BF16)]
    return pl.pallas_call(
        functools.partial(block_body, n_dev, group),
        out_shape=tuple(pltpu.VMEM(*t) for t in shapes) + tuple(sds(*t) for t in held),
        in_specs=[VM] * 4 + [HBM] * 6,
        out_specs=(VM,) * len(shapes) + (HBM,) * len(held),
        scratch_shapes=[
            vm((n_tok, width), BF16), vm((width, n_tok), BF16), vm((n_dev, seq, cols), BF16), vm((n_dev, seq, cols), BF16),
            vm((n_seq, n_rows), BF16), vm((n_rows, n_seq), BF16), vm((half, n_batch * n_seq), BF16), vm((group, 8, n_seq), F32), vm((n_seq, n_rows), BF16),
            vm((head_dim, n_seq), BF16), vm((head_dim, n_seq), BF16), vm((n_seq, head_dim), F32), vm((n_seq, head_dim), F32),
            vm((quarter, n_seq), F32), vm((quarter, n_seq), F32), vm((3, n_tok, head_dim), F32), vm((n_dev, n_batch, seq), jnp.int32),
            vm((2, seq, cols), BF16), vm((2, half, n_tok), BF16), vm((2, seq, n_rows), BF16),
            vm((n_batch, n_dev, seq, cols), BF16), vm((2, 8, width), F32), vm((n_dev, 2, width), F32),
            dma((15,)), dma((15,)), dma((9,)), dma((n_dev + 2,)), dma((9,)), dma((n_dev + 2,)), dma((9,)), dma((n_dev + 2,)), dma((n_dev,)), dma((n_dev,)), dma((2,)),
            dma((2, chips)), dma((2, chips)), dma((2, 2)), dma((2, 2)), dma((1 + 4 * chips,)), dma((1 + 4 * chips,)), dma((n_dev,)), dma((n_dev,)),
            dma((1 + n_dev,)), dma((3,)), dma((n_batch * n_dev,)), dma((W_SLOTS, 2)), dma((3, n_batch, 2)),
        ],
        compiler_params=pltpu.CompilerParams(collective_id=0, has_side_effects=True, vmem_limit_bytes=VMEM_LIMIT),
        cost_estimate=pl.CostEstimate(flops=10 ** 11, bytes_accessed=10 ** 8, transcendentals=0),
        name='block',
    )(gain, bias, positions, freq, x.reshape(n_tok, width), dy, wq, wk, wv, wo)[:len(shapes)]


def settle_body(n, *refs):
    sems = refs[2 * n]
    copies = [pltpu.make_async_copy(refs[i], refs[n + i], sems.at[i]) for i in range(n)]
    for copy in copies:
        copy.start()
    for copy in copies:
        copy.wait()


def settle(arrays):
    n = len(arrays)
    return pl.pallas_call(
        functools.partial(settle_body, n),
        out_shape=tuple(sds(t.shape, t.dtype) for t in arrays),
        in_specs=[ANY] * n,
        out_specs=(HBM,) * n,
        scratch_shapes=[pltpu.SemaphoreType.DMA((n,))],
        compiler_params=pltpu.CompilerParams(vmem_limit_bytes=1024 * 1024),
        name='settle',
    )(*arrays)


def solution(mesh):
    n_dev = mesh.shape['cp']

    def device_step(x_act, d_out, positions, ln_gain, ln_bias, w_query, w_key, w_value, w_out):
        n_batch, seq, width = x_act.shape
        q_heads, (kv_heads, head_dim) = w_query.shape[1], w_key.shape[1:]
        group = q_heads // kv_heads
        quarter = head_dim // 4
        assert n_batch == CORES and n_dev // CORES == kv_heads == 4 and q_heads * head_dim == width

        freq = np.exp(np.arange(quarter) * (-2.0 * math.log(ROPE_BASE) / (head_dim // 2))).astype(np.float32).reshape(quarter, 1)
        by_head = lambda t: jnp.transpose(t, (1, 0, 2))
        by_row = lambda t: t.reshape(width * kv_heads, head_dim)
        wq = by_head(w_query)

        results = whole_block(n_dev, x_act, ln_gain, ln_bias, positions, jnp.asarray(freq), d_out, wq, by_row(w_key), by_row(w_value), w_out)
        out, dx, dwq, dwk, dwv, dwo, dgain, dbias = settle(results)
        kv_rows = lambda t: t.reshape(width // n_dev, kv_heads, head_dim)
        return (out.reshape(x_act.shape), dx.reshape(x_act.shape), by_head(dwq), kv_rows(dwk), kv_rows(dwv), dwo, dgain, dbias)

    return jax.shard_map(device_step, mesh=mesh, in_specs=(P('dp', 'cp', None), P('dp', 'cp', None), P('dp', 'cp'), P(None), P(None), P(None, None, None), P(None, None, None), P(None, None, None), P(None, None)), out_specs=(P('dp', 'cp', None), P('dp', 'cp', None), P(('dp', 'cp'), None, None), P(('dp', 'cp'), None, None), P(('dp', 'cp'), None, None), P(('dp', 'cp'), None), P('dp'), P('dp')), check_vma=False)
```

time: 249 us -> 239 us (0.960)
  local copies, waits for them, and re-layouts: 15.1 us -> 0 us
  Pallas kernels: 233 us -> 238 us
    unnamed x22 -> x0, local copies, waits for them, and re-layouts: 15.1 us -> none
    pallas_call x2, Pallas kernels: 233 us -> 238 us  [the longest x1 231 us: whole_block(): pl.pallas_call(functools.partial(block_body, n_dev, group), out_shape=tup...]
where the time goes in v4:
time: 239 us; the launch traced here: 238 us
  Pallas kernels  238 us (100%)
    pallas_call x1, Pallas kernels, whole_block(): pl.pallas_call(functools.partial(block_body, n_dev, group), out_shape=tup...  231 us
    pallas_call x1, Pallas kernels, settle(): pl.pallas_call(functools.partial(settle_body, n), out_shape=tuple((sds(t....  6.7 us

profile of v4, /device:TPU:81, one launch (start us, length us, event | category | flops | bytes accessed | tf_op | source)
XLA Modules:
  0.0 238.4 jit_solution(7439053918898450724)
XLA Ops:
  0.6 230.9 %block.1 = (bf16[256,3584]{1,0:T(8,128)(2,1)S(1)}, bf16[256,3584]{1,0:T(8,128)(2,1)S(1)}, f32[28,448,128]{2,1,0:T(8,128)S(1)}, f32[1792,128]{1,0:T(8,128)S(1)}, ...) custom-call(f32[3584]{0:T(1024)} %gain_ref.1, ...), custom_call_target="tpu_custom_call" | custom-call | flops 99999997952 | bytes 100000000 | tf_op jit(solution)/shard_map/block/pallas_call | solution.py:616
  231.6 6.7 %settle.1 = (bf16[256,3584]{1,0:T(8,128)(2,1)}, bf16[256,3584]{1,0:T(8,128)(2,1)}, f32[28,448,128]{2,1,0:T(8,128)}, f32[1792,128]{1,0:T(8,128)}, f32[1792,128]{1...) custom-call(bf16[256,3584]{1,0:T(8,128)(2,1)S(1)} %get-tuple-element.24.refs_0_, ...), custom_call_target="tpu_custom_call" | custom-call | tf_op jit(solution)/shard_map/settle/pallas_call | solution.py:649
